TPU v7x, 256 devices: a whole 4x4x8 slice. The times are simulated.
256 devices in a mesh: gx: 4 (over y), gy: 8 (over x, core), gz: 8 (over z).
Axes of the slice: x: 4, y: 4, z: 8, core: 2. Of those that a mesh axis runs over, the one named last changes fastest.
Arguments:
- flow_state: float32 [5, 256, 128, 512], P(None, 'gz', 'gy', 'gx'), may hold values from -5 to 120, as said below
- advection: float32 [3, 5], replicated, may hold values from -400 to 400, as said below
- inverse_x: float32 [5, 128, 128], replicated, may hold values from -1 to 1, as said below
- inverse_y: float32 [5, 16, 16], replicated, may hold values from -1 to 1, as said below
- inverse_z: float32 [5, 32, 32], replicated, may hold values from -1 to 1, as said below
- reduced_x: float32 [5, 16, 16], replicated, as said below
- reduced_y: float32 [5, 32, 32], replicated, as said below
- reduced_z: float32 [5, 32, 32], replicated, as said below
Outputs:
- update: float32 [5, 256, 128, 512], P(None, 'gz', 'gy', 'gx')
- rms_norm: float32 [5], replicated
Inputs may be any that keep to these rules, and one draw needn't show every extreme that they name: flow_state[0] (density) lies between 0.5 and 2, and flow_state[4] / density minus half the squared velocity is at least 0.6 in every cell. `advection`: every entry has magnitude between 100 and 400. inverse_x[v] is the inverse of the 128 x 128 matrix with 4 on the diagonal, advection[0, v] / 2 - 2 just above it, -advection[0, v] / 2 - 2 just below it and 0.5 two places off it. inverse_y[v] is the inverse of the 16 x 16 matrix built likewise from advection[1, v]. inverse_z[v] is the inverse of the 32 x 32 matrix built likewise from advection[2, v]. reduced_x[v] is the inverse of I + K, K being the boundary rows and columns of the block inverses times the coupling between blocks, so that S_x equals the exact solution of the banded system along whole x lines with nothing beyond the grid's ends. reduced_y[v] is built likewise for y lines. reduced_z[v] is built likewise for z lines.
All inputs are finite; a program needn't handle non-finite values.
Results may differ from a plain program's by a relative error of at most 0.0002.
Values sent between devices are 32-bit elements.
No kernel may reach another device: no remote copies, remote signals or barrier semaphores. Data moves between devices by JAX's collectives and lax.ppermute only.
A program may use at most 64 MiB of HBM per device.

v0:
```python
import jax
import jax.numpy as jnp
from jax import lax
from jax.experimental import pallas as pl
from jax.experimental.pallas import tpu as pltpu
from jax.sharding import PartitionSpec as P


VARS = 5
F32 = jnp.float32
BF16 = jnp.bfloat16
DAMP = 0.0625
COURANT = 8000.0
VMEM = pltpu.VMEM
NN = (((1,), (0,)), ((), ()))


def iota(shape, dim):
    return lax.broadcasted_iota(jnp.int32, shape, dim)


def picks(shape, cond):
    return jnp.where(cond(iota(shape, 0), iota(shape, 1)), 1.0, 0.0).astype(BF16)


def split(x):
    hi = x.astype(BF16)
    return hi, (x - hi.astype(F32)).astype(BF16)


def dot1(a, b, dims=NN):
    return lax.dot_general(a, b, dims, preferred_element_type=F32)


def stacked(x):
    hi, lo = split(x)
    return jnp.concatenate([hi, hi, lo], axis=0)


def small_solve(table, pieces):
    return dot1(table, stacked(jnp.concatenate(pieces, axis=0)))


def call(body, out, args, scratch=(), far=(), smem=(), far_out=(), smem_out=(), sems=0, limit=24, flops=1_000_000):
    def spec(k, places):
        if k in smem and places is far:
            return pl.BlockSpec(memory_space=pltpu.SMEM)
        return pl.BlockSpec(memory_space=pltpu.HBM if k in places else VMEM)

    size = sum(a.size * a.dtype.itemsize for a in args)
    shapes = [VMEM(*t) for t in scratch]
    if sems:
        shapes.append(pltpu.SemaphoreType.DMA((sems,)))
    return pl.pallas_call(
        body,
        out_shape=[jax.ShapeDtypeStruct(*o) for o in out],
        in_specs=[spec(k, far) for k in range(len(args))],
        out_specs=[
            pl.BlockSpec(memory_space=pltpu.SMEM if k in smem_out else pltpu.HBM if k in far_out else VMEM)
            for k in range(len(out))
        ],
        scratch_shapes=shapes,
        compiler_params=pltpu.CompilerParams(vmem_limit_bytes=limit * 1024 * 1024),
        cost_estimate=pl.CostEstimate(flops=flops, bytes_accessed=size, transcendentals=0),
    )(*args)


def spread(left, parts, right, keep=None):
    wide = [dot1(dot1(left, part).astype(BF16), right) for part in parts]
    if keep is not None:
        wide = [jnp.where(keep, x, 0.0) for x in wide]
    return [x.astype(BF16) for x in wide]


def masked(shape, cond):
    return cond(iota(shape, 0), iota(shape, 1))


def put(ref, v, halves):
    hi, lo = halves
    k = hi.shape[1]
    ref[v, :, 0:k] = hi
    ref[v, :, k : 2 * k] = lo
    ref[v, :, 2 * k : 3 * k] = hi


def solve_tables_body(invy, invz, ay, az):
    y_left = picks((128, 16), lambda a, k: (a & 15) == k)
    y_right = picks((16, 128), lambda k, c: k == (c & 15))
    y_same = masked((128, 128), lambda a, c: (a >> 4) == (c >> 4))
    z_left = picks((256, 32), lambda a, k: (a >> 3) == k)
    z_right = picks((32, 256), lambda k, c: k == (c >> 3))
    z_same = masked((256, 256), lambda a, c: (a & 7) == (c & 7))
    for v in range(VARS):
        put(ay, v, spread(y_left, split(invy[v]), y_right, y_same))
        put(az, v, spread(z_left, split(invz[v]), z_right, z_same))


def first_off(r):
    return r - 2 + 4 * (r >> 1)


def second_off(r):
    return jnp.where(r == 0, -1, jnp.where(r == 3, 4, -4096))


def near(chosen, red, row, speed):
    hi, lo = split(red)
    both = dot1(chosen, hi) + dot1(chosen, lo)
    rows = both.shape[0] // 2
    other = jnp.where(row == 0, -0.5 * speed - 2.0, jnp.where(row == 3, 0.5 * speed - 2.0, 0.0))
    return 0.5 * both[0:rows] + other * both[rows:]


def exact(a, b):
    return lax.dot_general(a, b, NN, precision=lax.Precision.HIGHEST, preferred_element_type=F32)


def send_tables(adv, redx, redy, redz, nx, ty, tz):
    ix, iy, iz = lax.axis_index("gx"), lax.axis_index("gy"), lax.axis_index("gz")
    same = masked((32, 32), lambda a, c: (a & 7) == (c & 7))
    for out, red, at in ((ty, redy, iy), (tz, redz, iz)):
        left = picks((32, 32), lambda a, k: k == 4 * at + (a >> 3))
        right = picks((32, 32), lambda k, c: k == 4 * at + (c >> 3))
        for v in range(VARS):
            put(out, v, spread(left, split(red[v]), right, same))
    total = None
    row = (iota((32, 16), 0) & 3) ^ 2
    for v in range(VARS):
        chosen = jnp.concatenate(
            [
                picks((32, 16), lambda a, k, f=f: ((a >> 2) == v) & (k == 4 * ix + f((a & 3) ^ 2)))
                for f in (first_off, second_off)
            ],
            axis=0,
        )
        term = near(chosen, redx[v], row, adv[0, v])
        total = term if total is None else total + term
    right = picks((16, 128), lambda k, c: k == 4 * ((ix + 4 - (c >> 5)) & 3) + ((c & 3) ^ 2))
    same = masked((32, 128), lambda a, c: (a >> 2) == ((c >> 2) & 7))
    hi, lo = [jnp.where(same, dot1(part, right), 0.0).astype(BF16) for part in split(total)]
    nx[:, 0:128] = hi
    nx[:, 128:256] = lo
    nx[:, 256:384] = hi


def take_tables(adv, redy, redz, my, mz, ny, wide):
    row, lane = iota((32, 160), 0), iota((32, 160), 1)
    block, first = (lane >> 2) & 7, row - (lane & 28)
    low = (iota((8, 160), 0) & 3) < 2
    same = jnp.where((iota((160, 160), 0) >> 2) == (iota((160, 160), 1) >> 2), 1.0, 0.0)
    keep = masked((32, 432), lambda a, c: (a & 7) == (c & 7))
    left = picks((32, 8), lambda a, k: k == (a >> 3))
    third = iota((32, 432), 1)
    third, spot = jnp.where(third < 144, 0, jnp.where(third < 288, 1, 2)), third
    spot = (spot - 144 * third) >> 3
    spot = jnp.where(iota((32, 432), 0) == spot, 1.0, 0.0)
    ends, inner = jnp.where(third == 1, 0.0, spot).astype(BF16), jnp.where(third == 1, spot, 0.0).astype(BF16)
    source, column = iota((640, 160), 0), iota((640, 160), 1)
    part = jnp.where(source < 160, 0, jnp.where(source < 320, 1, jnp.where(source < 480, 2, 3)))
    inside = source - 160 * part
    for out, red, d, axis in ((my, redy, 1, "gy"), (mz, redz, 2, "gz")):
        at = lax.axis_index(axis)
        flip = at if axis == "gy" else 0
        for v in range(VARS):
            wide[:, 32 * v : 32 * v + 32] = red[v]
        table = wide[:, 0:160]
        start = jnp.where(block < at, 2, 0)
        here = block[0:8] == at

        def line(which):
            return jnp.sum(jnp.where(which, table, 0.0), axis=0, keepdims=True)

        a0, a1 = line(first == start), line(first == start + 1)
        e0, e1 = line(first == 2), line(first == 3)
        blank = jnp.zeros((2, 160), F32)
        sums = exact(jnp.concatenate([a0 * a0, a0 * a1, a1 * a1, e0 * e0, e0 * e1, e1 * e1, blank], axis=0), same)

        def dual(u0, u1, g):
            scale = 1.0 / (g[0:1] * g[2:3] - g[1:2] * g[1:2])
            return (g[2:3] * u0 - g[1:2] * u1) * scale, (g[0:1] * u1 - g[1:2] * u0) * scale

        p0, p1 = dual(a0, a1, sums[0:3])
        f0, f1 = dual(e0, e1, sums[3:6])
        chosen = jnp.concatenate(
            [picks((8, 32), lambda a, k, f=f: k == 4 * at + f(a & 3)) for f in (first_off, second_off)], axis=0
        )
        speed = jnp.zeros((8, 160), F32)
        for v in range(VARS):
            speed = jnp.where((iota((8, 160), 1) >> 5) == v, adv[d, v], speed)
        needed = near(chosen, table, iota((8, 160), 0) & 3, speed)
        sent = jnp.where(here & ~low, 0.0, needed)
        own = jnp.where(here & ~low, needed, 0.0)
        place = jnp.where(part < 2, 2 * (((inside >> 2) & 7) ^ flip), 14) + part
        gather = jnp.where(column == (inside & 224) + place, 1.0, 0.0)
        found = exact(jnp.concatenate([sent * p0, sent * p1, own * f0, own * f1], axis=1), gather)
        hi, lo = [dot1(left, x).astype(BF16) for x in split(found)]
        for v in range(VARS):
            at_v = slice(32 * v, 32 * v + 32)
            out[v] = jnp.where(keep, dot1(hi[:, at_v], ends) + dot1(lo[:, at_v], inner), 0.0).astype(BF16)
        if axis == "gy":
            wanted = iota((32, 96), 0) == 4 * (at ^ ((iota((32, 96), 1) >> 2) & 7)) + (iota((32, 96), 1) & 3)
            second = (iota((32, 96), 1) >> 5) == 1
            y_ends = jnp.where(wanted & ~second, 1.0, 0.0).astype(BF16)
            y_inner = jnp.where(wanted & second, 1.0, 0.0).astype(BF16)
            hi, lo = [jnp.concatenate([x, x], axis=0) for x in split(needed)]
            for v in range(VARS):
                at_v = slice(32 * v, 32 * v + 32)
                ny[v] = (dot1(hi[:, at_v], y_ends) + dot1(lo[:, at_v], y_inner)).astype(BF16)


def window_tables_body(adv, redx, redy, redz, invy, invz, nx, ty, tz, my, mz, ny, qy, qz, qzy, wide):
    send_tables(adv, redx, redy, redz, nx, ty, tz)
    take_tables(adv, redy, redz, my, mz, ny, wide)
    column_tables(invy, invz, qy, qz, qzy)


def column_tables(invy, invz, qy, qz, qzy):
    y_left = picks((128, 16), lambda a, k: (a & 15) == k)
    y_right = picks((16, 32), lambda k, c: k == (c >> 3) + 12 * (c >> 4))
    y_same = masked((128, 32), lambda a, c: (a >> 4) == (c & 7))
    z_left = picks((256, 32), lambda a, k: (a >> 3) == k)
    z_right = picks((32, 32), lambda k, c: k == (c >> 3) + 28 * (c >> 4))
    z_same = masked((256, 32), lambda a, c: (a & 7) == (c & 7))
    zy_left = picks((128, 32), lambda a, k: k == 8 * (a >> 5) + (a & 7))
    zy_right = picks((32, 16), lambda k, c: k == (c >> 2) + 28 * (c >> 3))
    zy_same = masked((128, 16), lambda a, c: ((a >> 3) & 3) == (c & 3))
    for v in range(VARS):
        put(qy, v, spread(y_left, split(invy[v]), y_right, y_same))
        parts = split(invz[v])
        put(qz, v, spread(z_left, parts, z_right, z_same))
        put(qzy, v, spread(zy_left, parts, zy_right, zy_same))


def faces_body(u, xlo, xhi, ylo, yhi, zlo, zhi):
    lane = iota((512, 128), 1)
    wide = jnp.zeros((512, 128), F32)
    for v in range(VARS):
        block = u[512 * v : 512 * v + 512, :]
        low = pltpu.roll(block, 2 * v, 1) if v else block
        wide = jnp.where((lane >> 1) == v, low, wide)
        wide = jnp.where((lane >> 1) == 8 + v, pltpu.roll(block, 18 + 2 * v, 1), wide)
        for j in range(2):
            at = 32 * (2 * v + j)
            ylo[at : at + 32, :] = u[pl.ds(512 * v + j, 32, stride=16), :]
            yhi[at : at + 32, :] = u[pl.ds(512 * v + 14 + j, 32, stride=16), :]
        zlo[32 * v : 32 * v + 32, :] = u[512 * v : 512 * v + 32, :]
        zhi[32 * v : 32 * v + 32, :] = u[512 * v + 480 : 512 * v + 512, :]
    turned = wide.T
    xlo[...] = turned[0:16]
    xhi[...] = turned[16:32]


def primitives(u):
    inverse = 1.0 / u[0]
    velocity = [u[1 + k] * inverse for k in range(3)]
    kinetic = 0.5 * (velocity[0] * velocity[0] + velocity[1] * velocity[1] + velocity[2] * velocity[2])
    internal = jnp.maximum(u[4] * inverse - kinetic, 0.25)
    return velocity, internal, 0.4 * u[0] * internal


def flux(u, velocity, pressure, d):
    w = velocity[d]
    out = [u[1 + d]]
    for k in range(3):
        moment = u[1 + k] * w
        out.append(moment + pressure if k == d else moment)
    out.append((u[4] + pressure) * w)
    return out


def stats_row(shape, sums, top):
    lane = iota(shape, len(shape) - 1)
    row = jnp.where(lane == VARS, top, 0.0)
    for v in range(VARS):
        row = jnp.where(lane == v, sums[v], row)
    return row


def merged_stats(rows):
    lane = iota(rows[0].shape, 1)
    total, top = rows[0], rows[0]
    for row in rows[1:]:
        total, top = total + row, jnp.maximum(top, row)
    return jnp.where(lane < VARS, total, top)


def residual_body(
    u, xlo, xhi, ylo, yhi, zlo, zhi, own_lo, own_hi, invx, ay, az, w, bx, qx, pad, fy, fz, res, fix, half, edge
):
    def fill(z, carry):
        for v in range(VARS):
            pad[36 * v + 2 + z, 8:24, :] = u[pl.ds(pl.multiple_of(512 * v + 16 * z, 16), 16), :]
        return carry

    lax.fori_loop(0, 32, fill, 0)
    rows = pad.reshape(180 * 32, 128)
    for v in range(VARS):
        for k in range(2):
            pad[36 * v + k, 8:24, :] = zlo[32 * v + 16 * k : 32 * v + 16 * k + 16, :]
            pad[36 * v + 34 + k, 8:24, :] = zhi[32 * v + 16 * k : 32 * v + 16 * k + 16, :]
            at = 32 * (2 * v + k)
            rows[pl.ds(32 * (36 * v + 2) + 6 + k, 32, stride=32), :] = ylo[at : at + 32, :]
            rows[pl.ds(32 * (36 * v + 2) + 24 + k, 32, stride=32), :] = yhi[at : at + 32, :]

    edge[...] = jnp.zeros_like(edge)

    def line(ref, j):
        return [ref[2 * v + j : 2 * v + j + 1, :] for v in range(VARS)]

    def fx(u):
        velocity, _, pressure = primitives(u)
        return flux(u, velocity, pressure, 0)

    l2, l1, h1, h2 = line(xlo, 0), line(xlo, 1), line(xhi, 0), line(xhi, 1)
    o0, o1, p1, p0 = line(own_lo, 0), line(own_lo, 1), line(own_hi, 0), line(own_hi, 1)
    fl, fp, fh, fo = fx(l1), fx(p0), fx(h1), fx(o0)
    for v in range(VARS):
        dl, dh = l1[v] - p0[v], h1[v] - o0[v]
        edge[4 * v : 4 * v + 1, :] = -DAMP * dh
        edge[4 * v + 1 : 4 * v + 2, :] = -0.5 * (fh[v] - fo[v]) + 4.0 * DAMP * dh - DAMP * (h2[v] - o1[v])
        edge[4 * v + 2 : 4 * v + 3, :] = 0.5 * (fl[v] - fp[v]) + 4.0 * DAMP * dl - DAMP * (l2[v] - p1[v])
        edge[4 * v + 3 : 4 * v + 4, :] = -DAMP * dl
    fix[...] = edge[...].T

    for z in (-1, 32):
        c = [pad[36 * v + 2 + z, 8:24, :] for v in range(VARS)]
        velocity, _, pressure = primitives(c)
        for v, f in enumerate(flux(c, velocity, pressure, 2)):
            fz[34 * v + 1 + z] = f

    def plane(z, top):
        full = [pad[36 * v + 2 + z] for v in range(VARS)]
        velocity, internal, pressure = primitives(full)
        for v, f in enumerate(flux(full, velocity, pressure, 1)):
            fy[32 * v + z] = f
        c = [f[8:24] for f in full]
        velocity, internal, pressure = [f[8:24] for f in velocity], internal[8:24], pressure[8:24]
        for v, f in enumerate(flux(c, velocity, pressure, 2)):
            fz[34 * v + 1 + z] = f
        for v, f in enumerate(flux(c, velocity, pressure, 0)):
            damped = (4.0 * DAMP) * c[v]
            res[32 * v + z] = (
                pltpu.roll(damped - 0.5 * f, 127, 1)
                + pltpu.roll(damped + 0.5 * f, 1, 1)
                - DAMP * (pltpu.roll(c[v], 126, 1) + pltpu.roll(c[v], 2, 1))
                - (18.0 * DAMP) * c[v]
            )
        speed = jnp.abs(velocity[0]) + jnp.abs(velocity[1]) + jnp.abs(velocity[2])
        return jnp.maximum(top, speed + jnp.sqrt((3.0 * 1.4 * 0.4) * internal))

    top = lax.fori_loop(0, 32, plane, jnp.zeros((16, 128), F32), unroll=2)

    lane = iota((16, 128), 1)
    edges = (lane < 2) | (lane >= 126)

    def finish(z, sums):
        out = []
        fixes = fix[pl.ds(pl.multiple_of(16 * z, 16), 16), :]
        for v in range(VARS):
            at = 36 * v + 2 + z
            ones = (pad[at, 7:23, :] + pad[at, 9:25, :]) + (pad[at - 1, 8:24, :] + pad[at + 1, 8:24, :])
            twos = (pad[at, 6:22, :] + pad[at, 10:26, :]) + (pad[at - 2, 8:24, :] + pad[at + 2, 8:24, :])
            steep = (fy[32 * v + z, 7:23, :] - fy[32 * v + z, 9:25, :]) + (fz[34 * v + z] - fz[34 * v + 2 + z])
            value = res[32 * v + z] + 0.5 * steep + (4.0 * DAMP) * ones - DAMP * twos
            value = value + jnp.where(edges, pltpu.roll(fixes, (126 - 4 * v) & 127, 1), 0.0)
            res[32 * v + z] = value
            out.append(sums[v] + value * value)
        return tuple(out)

    sums = lax.fori_loop(0, 32, finish, tuple(jnp.zeros((16, 128), F32) for _ in range(VARS)), unroll=2)

    qx[...] = jnp.zeros_like(qx)
    for v in range(VARS):
        turned = invx[v].T
        qx[4 * v : 4 * v + 2, :] = turned[126:128]
        qx[4 * v + 2 : 4 * v + 4, :] = turned[0:2]
        hi, lo = split(res[pl.ds(32 * v, 32)].reshape(512, 128))
        half[...] = dot1(jnp.concatenate([hi, lo, hi], axis=1), stacked(turned))
        for g in range(4):
            half[128 * g : 128 * g + 128, :] = dot1(ay[v], stacked(half[128 * g : 128 * g + 128, :]))
        field = half[...].reshape(32, 2, 8, 128)
        parts = [dot1(az[v], stacked(field[:, h].reshape(256, 128))).reshape(32, 1, 8, 128) for h in range(2)]
        w[pl.ds(pl.multiple_of(512 * v, 512), 512), :] = jnp.concatenate(parts, axis=1).reshape(512, 128)
    lane = iota((512, 128), 1)
    wide = jnp.zeros((512, 128), F32)
    for v in range(VARS):
        wide = jnp.where((lane >> 2) == v, pltpu.roll(w[512 * v : 512 * v + 512, :], 2 + 4 * v, 1), wide)
    turned = wide.T
    bx[...] = turned[0:24]
    bx[20:21, :] = stats_row((1, 512), [jnp.sum(s) for s in sums], jnp.max(top))


def spread_body(w, b0, b1, b2, b3, nx, qx, ty, tz, *rest):
    far, (mine, ydown, yup), towards, (v1, zp, wide, sem) = rest[:2], rest[2:5], rest[5:9], rest[9:]
    me, iz = lax.axis_index("gy"), lax.axis_index("gz")
    ups = [(me & 1) == 0] + [((me >> 1) ^ j) > (me >> 1) for j in (1, 2, 3)]
    blank = jnp.zeros((8, 512), F32)
    pieces = [b0, b1, b2, b3]
    data = jnp.concatenate([t for p in pieces for t in (p[...], blank)], axis=0)
    wide[...] = jnp.zeros_like(wide)
    wide[0:32, :] = dot1(nx[...], stacked(data))
    hi, lo = split(wide[...].T[:, 0:32])
    turned = jnp.concatenate([hi, lo, hi], axis=1)
    copies = []
    for v in range(VARS):
        at = pl.ds(512 * v, 512)
        hi, lo = split(jnp.where((iota((32, 128), 0) >> 2) == v, qx[...], 0.0))
        v1[at, :] = w[at, :] - dot1(turned, jnp.concatenate([hi, hi, lo], axis=0))
        copies.append(pltpu.make_async_copy(v1.at[at], far[0].at[at], sem.at[v]))
        copies[-1].start()
        for h in range(2):
            ends = [v1[512 * v + 16 * z + 8 * h : 512 * v + 16 * z + 8 * h + 8, :] for z in (0, 1, 30, 31)]
            sent = small_solve(tz[v], ends)
            at = 16 * (2 * v + h)
            mine[at : at + 16, :] = sent[16:32]
            for p in range(8):
                zp[p, at : at + 16, :] = jnp.where(p <= iz, sent[0:16], sent[16:32])
        for t in range(4):
            sent = small_solve(ty[v], [v1[pl.ds(512 * v + 128 * t + y, 8, stride=16), :] for y in (0, 1, 14, 15)])
            at = 16 * (4 * v + t)
            ydown[at : at + 16, :] = sent[0:16]
            yup[at : at + 16, :] = sent[16:32]
            for up, out in zip(ups, towards):
                out[at : at + 16, :] = jnp.where(up, sent[16:32], sent[0:16])
        at = pl.ds(32 * v, 32)
        copies.append(pltpu.make_async_copy(zp.at[:, at], far[1].at[:, at], sem.at[5 + v]))
        copies[-1].start()
    stats = jnp.broadcast_to(merged_stats([p[20:21, 0:128] for p in pieces]), (8, 128))
    for p in range(8):
        zp[p, 160:168, :] = stats
    at = pl.ds(160, 8)
    copies.append(pltpu.make_async_copy(zp.at[:, at], far[1].at[:, at], sem.at[10]))
    copies[-1].start()
    for c in copies:
        c.wait()


def cross_body(zr, mine, mz, *refs):
    zy, zc = refs[-2:]
    for v in range(VARS):
        for h in range(2):
            at = 16 * (2 * v + h)
            got = [zr[168 * q + at : 168 * q + at + 16, :] for q in range(8)] + [mine[at : at + 16, :]]
            zc[2 * at : 2 * at + 32, :] = small_solve(mz[v], got)
        for j, (h, y) in enumerate(((0, 0), (0, 1), (1, 6), (1, 7))):
            zy[pl.ds(16 * v + j, 4, stride=4), :] = zc[pl.ds(32 * (2 * v + h) + y, 4, stride=8), :]
    zy[80:88, :] = merged_stats([zr[168 * q + 160 : 168 * q + 168, :] for q in range(8)])


def middle_y_body(v1_far, my, qy, *refs):
    lines, (vy_far, v1, vy, sem) = refs[:9], refs[9:]
    copies, puts = [], []
    for v in range(VARS):
        at = pl.ds(512 * v, 512)
        copies.append(pltpu.make_async_copy(v1_far.at[at], v1.at[at], sem.at[v]))
        puts.append(pltpu.make_async_copy(vy.at[at], vy_far.at[at], sem.at[5 + v]))
        copies[v].start()
    for v in range(VARS):
        copies[v].wait()
        for t in range(4):
            at = 16 * (4 * v + t)
            found = small_solve(my[v], [x[at : at + 16, :] for x in lines])
            at = pl.ds(512 * v + 128 * t, 128)
            vy[at, :] = v1[at, :] - dot1(qy[v], stacked(found))
        puts[v].start()
    for c in puts:
        c.wait()


def middle_z_body(vy_far, zc, qz, v2, vy, sem):
    copies = []
    for v in range(VARS):
        at = pl.ds(512 * v, 512)
        copies.append(pltpu.make_async_copy(vy_far.at[at], vy.at[at], sem.at[v]))
        copies[v].start()
    for v in range(VARS):
        parts = []
        for h in range(2):
            rows = zc[64 * v + 32 * h : 64 * v + 32 * h + 32, :]
            parts.append(dot1(qz[v], stacked(rows)).reshape(32, 1, 8, 128))
        planes = jnp.concatenate(parts, axis=1).reshape(512, 128)
        copies[v].wait()
        at = pl.ds(512 * v, 512)
        v2[at, :] = vy[at, :] - planes


def last_body(v2, *refs):
    zr, (ny, qzy, qy, out_far, fin, out, sem) = refs[:8], refs[8:]
    stats = merged_stats([r[80:88, :] for r in zr])
    lane = iota((8, 128), 1)
    step = COURANT / jnp.max(jnp.where(lane == VARS, stats, 0.0))
    norm = jnp.sqrt(stats * (1.0 / 16777216.0))
    for v in range(VARS):
        fin[v] = jnp.max(jnp.where(lane == v, norm, 0.0))
    copies = []
    for v in range(VARS):
        table = ny[v]
        crossed = jnp.concatenate(
            [small_solve(table, [x[16 * v + 4 * r : 16 * v + 4 * r + 4, :] for x in zr])[0:4] for r in range(4)], axis=0
        )
        lines = dot1(qzy[v], stacked(crossed))
        for t in range(4):
            at = pl.ds(512 * v + 128 * t, 128)
            out[at, :] = step * (v2[at, :] + dot1(qy[v], stacked(lines[32 * t : 32 * t + 32])))
        at = pl.ds(512 * v, 512)
        copies.append(pltpu.make_async_copy(out.at[at], out_far.at[at], sem.at[v]))
        copies[v].start()
    for c in copies:
        c.wait()


def handed(x, axis):
    return lax.all_to_all(x, axis, 0, 0, tiled=True)


def shifted(x, axis, by):
    size = lax.axis_size(axis)
    return lax.ppermute(x, axis, [(i, (i + by) % size) for i in range(size)])


def swapped(x, axis, k):
    return lax.ppermute(x, axis, [(i, i ^ k) for i in range(lax.axis_size(axis))])


def step(flow_state, advection, inverse_x, inverse_y, inverse_z, reduced_x, reduced_y, reduced_z):
    u = flow_state.reshape(2560, 128)
    xlo, xhi, ylo, yhi, zlo, zhi = call(
        faces_body, [((16, 512), F32)] * 2 + [((320, 128), F32)] * 2 + [((160, 128), F32)] * 2, (u,)
    )
    from_zlo, from_zhi = shifted(zhi, "gz", 1), shifted(zlo, "gz", -1)
    from_ylo, from_yhi = shifted(yhi, "gy", 1), shifted(ylo, "gy", -1)
    from_xlo, from_xhi = shifted(xhi, "gx", 1), shifted(xlo, "gx", -1)
    ay, az = call(solve_tables_body, [((5, 128, 384), BF16), ((5, 256, 768), BF16)], (inverse_y, inverse_z))
    w, bx, qx = call(
        residual_body,
        [((2560, 128), F32), ((24, 512), F32), ((32, 128), F32)],
        (u, from_xlo, from_xhi, from_ylo, from_yhi, from_zlo, from_zhi, xlo, xhi, inverse_x, ay, az),
        scratch=[
            ((180, 32, 128), F32),
            ((160, 32, 128), F32),
            ((170, 16, 128), F32),
            ((160, 16, 128), F32),
            ((512, 128), F32),
            ((512, 128), F32),
            ((128, 512), F32),
        ],
    )
    pieces = [bx] + [shifted(bx, "gx", k) for k in (1, 2, 3)]
    nx, ty, tz, my, mz, ny, qy, qz, qzy = call(
        window_tables_body,
        [
            ((32, 384), BF16),
            ((5, 32, 96), BF16),
            ((5, 32, 96), BF16),
            ((5, 32, 432), BF16),
            ((5, 32, 432), BF16),
            ((5, 16, 96), BF16),
            ((5, 128, 96), BF16),
            ((5, 256, 96), BF16),
            ((5, 128, 48), BF16),
        ],
        (advection, reduced_x, reduced_y, reduced_z, inverse_y, inverse_z),
        scratch=[((32, 256), F32)],
        smem=(0,),
    )
    big, tall, flat = ((2560, 128), F32), ((8, 168, 128), F32), ((320, 128), F32)
    v1, zp, mine, ydown, yup, pair, *chips = call(
        spread_body,
        [big, tall, ((160, 128), F32)] + [flat] * 6,
        (w, *pieces, nx, qx, ty, tz),
        scratch=[big, tall, ((128, 512), F32)],
        far_out=(0, 1),
        sems=11,
    )
    zr = handed(zp, "gz").reshape(1344, 128)
    lines = [ydown, swapped(pair, "gy", 1)]
    for j in (1, 2, 3):
        lines.append(swapped(chips[j - 1], "gy", 2 * j))
        lines.append(swapped(lines[-1], "gy", 1))
    lines.append(yup)
    (vy,) = call(
        middle_y_body,
        [big],
        (v1, my, qy, *lines),
        scratch=[big, big],
        far=(0,),
        far_out=(0,),
        sems=10,
    )
    zy, zc = call(
        cross_body, [((88, 128), F32), ((320, 128), F32)], (zr, mine, mz, vy), far=(3,)
    )
    crossed = [zy, swapped(zy, "gy", 1)]
    for k in (2, 4, 6):
        crossed.append(swapped(zy, "gy", k))
        crossed.append(swapped(crossed[-1], "gy", 1))
    (v2,) = call(middle_z_body, [big], (vy, zc, qz), scratch=[big], far=(0,), sems=5)
    out, fin = call(
        last_body,
        [((2560, 128), F32), ((VARS,), F32)],
        (v2, *crossed, ny, qzy, qy),
        scratch=[((2560, 128), F32)],
        far_out=(0,),
        smem_out=(1,),
        sems=5,
    )
    return out.reshape(5, 32, 16, 128), fin


def solution(mesh):
    spec = P(None, "gz", "gy", "gx")
    return jax.shard_map(
        step,
        mesh=mesh,
        in_specs=(spec, P(), P(), P(), P(), P(), P(), P()),
        out_specs=(spec, P()),
        check_vma=False,
    )
```

profile of v0, /device:TPU:41, one launch (start us, length us, event | category | flops | bytes accessed | tf_op | source)
XLA Modules:
  0.0 81.9 jit_solution(9075640585350021912)
XLA Ops:
  0.6 1.3 %copy-done = f32[5,32,16,128]{3,2,1,0:T(8,128)S(1)} copy-done((f32[5,32,16,128]{3,2,1,0:T(8,128)S(1)}, f32[5,32,16,128]{3,2,1,0:T(8,128)}, u32[]{:S(2)}) %copy-start) | copy-done | bytes 1310744
  2.7 1.8 %collective-permute-start.2 = (f32[320,128]{1,0:T(8,128)S(1)}, f32[320,128]{1,0:T(8,128)S(1)}, u32[]{:S(2)}, u32[]{:S(2)}) collective-permute-start(f32[320,128]{1,0:T(8,128)S(1)} %get-tuple-element.37), channel_id=1, source_target_pairs={{0,8},{8,16},{16,24},{24,32},{32,40},{40,48},{48,56},{56,0},{1,9},... | collective-permute-start | bytes 491528 | tf_op jit(solution)/shard_map/ppermute | solution.py:519
  4.5 1.6 %collective-permute-start.4 = (f32[160,128]{1,0:T(8,128)S(1)}, f32[160,128]{1,0:T(8,128)S(1)}, u32[]{:S(2)}, u32[]{:S(2)}) collective-permute-start(f32[160,128]{1,0:T(8,128)S(1)} %get-tuple-element.39), channel_id=1, source_target_pairs={{0,1},{1,2},{2,3},{3,4},{4,5},{5,6},{6,7},{7,0},{8,9},{9,10},{10,1... | collective-permute-start | bytes 245768 | tf_op jit(solution)/shard_map/ppermute | solution.py:519
  6.2 1.3 %collective-permute-start = (f32[16,512]{1,0:T(8,128)S(1)}, f32[16,512]{1,0:T(8,128)S(1)}, u32[]{:S(2)}, u32[]{:S(2)}) collective-permute-start(f32[16,512]{1,0:T(8,128)S(1)} %get-tuple-element.35.own_hi), channel_id=1, source_target_pairs={{0,64},{64,128},{128,192},{192,0},{1,65},{65,129},{129,193},{193,1... | collective-permute-start | bytes 98312 | tf_op jit(solution)/shard_map/ppermute | solution.py:519
  7.5 1.5 %collective-permute-done.xlo = f32[16,512]{1,0:T(8,128)S(1)} collective-permute-done((f32[16,512]{1,0:T(8,128)S(1)}, f32[16,512]{1,0:T(8,128)S(1)}, u32[]{:S(2)}, u32[]{:S(2)}) %collective-permute-start) | collective-permute-done | bytes 32800 | tf_op jit(solution)/shard_map/ppermute | solution.py:519
  9.0 1.4 %collective-permute-start.1 = (f32[16,512]{1,0:T(8,128)S(1)}, f32[16,512]{1,0:T(8,128)S(1)}, u32[]{:S(2)}, u32[]{:S(2)}) collective-permute-start(f32[16,512]{1,0:T(8,128)S(1)} %get-tuple-element.36.own_lo), channel_id=1, source_target_pairs={{0,192},{64,0},{128,64},{192,128},{1,193},{65,1},{129,65},{193,129... | collective-permute-start | bytes 98312 | tf_op jit(solution)/shard_map/ppermute | solution.py:519
  12.0 1.8 %shard_map.96 = (bf16[5,128,384]{2,1,0:T(8,128)(2,1)S(1)}, bf16[5,256,768]{2,1,0:T(8,128)(2,1)S(1)}) custom-call(f32[5,16,16]{2,1,0:T(8,128)S(1)} %copy-done.14, f32[5,32,32]{2,1,0:T(8,128)S(1)} %copy-done.5), custom_call_target="tpu_custom_call" | custom-call | flops 1000000 | bytes 25600 | tf_op jit(solution)/shard_map/pallas_call | solution.py:54
  14.9 8.3 %shard_map.97 = (f32[2560,128]{1,0:T(8,128)S(1)}, f32[24,512]{1,0:T(8,128)S(1)}, f32[32,128]{1,0:T(8,128)S(1)}) custom-call(f32[2560,128]{1,0:T(8,128)S(1)} %bitcast.4, f32[16,512]{1,0:T(8,128)S(1)} %collective-permute-done.xlo, f32[16,512]{1,0:T(8,128)S(1)} %collective-permute-done.1.xhi, f32[320,128]{1,0:T(8,128)S(1)} %collective-permute-done.2.ylo, ...), custom_call_target="tpu_custom_call" | custom-call | flops 1000000 | bytes 4718592 | tf_op jit(solution)/shard_map/pallas_call | solution.py:54
  23.2 1.6 %collective-permute-start.8 = (f32[24,512]{1,0:T(8,128)S(1)}, f32[24,512]{1,0:T(8,128)S(1)}, u32[]{:S(2)}, u32[]{:S(2)}) collective-permute-start(f32[24,512]{1,0:T(8,128)S(1)} %get-tuple-element.44.b0), channel_id=1, source_target_pairs={{0,192},{64,0},{128,64},{192,128},{1,193},{65,1},{129,65},{193,129... | collective-permute-start | bytes 147464 | tf_op jit(solution)/shard_map/ppermute | solution.py:519
  24.8 1.6 %collective-permute-start.6 = (f32[24,512]{1,0:T(8,128)S(1)}, f32[24,512]{1,0:T(8,128)S(1)}, u32[]{:S(2)}, u32[]{:S(2)}) collective-permute-start(f32[24,512]{1,0:T(8,128)S(1)} %get-tuple-element.44.b0), channel_id=1, source_target_pairs={{0,64},{64,128},{128,192},{192,0},{1,65},{65,129},{129,193},{193,1... | collective-permute-start | bytes 147464 | tf_op jit(solution)/shard_map/ppermute | solution.py:519
  26.4 5.2 %shard_map.98 = (bf16[32,384]{1,0:T(8,128)(2,1)S(1)}, bf16[5,32,96]{2,1,0:T(8,128)(2,1)S(1)}, bf16[5,32,96]{2,1,0:T(8,128)(2,1)S(1)}, bf16[5,32,432]{2,1,0:T(8,1...) custom-call(f32[3,5]{1,0:T(4,128)S(1)} %copy-done.22, ...), custom_call_target="tpu_custom_call" | custom-call | flops 1000000 | bytes 71740 | tf_op jit(solution)/shard_map/pallas_call | solution.py:54
  31.7 2.6 %shard_map.99 = (f32[2560,128]{1,0:T(8,128)S(1)}, f32[8,168,128]{2,1,0:T(8,128)}, f32[160,128]{1,0:T(8,128)S(1)}, f32[320,128]{1,0:T(8,128)S(1)}, f32[320,128]{1...) custom-call(f32[2560,128]{1,0:T(8,128)S(1)} %get-tuple-element.43.w,, ...), custom_call_target="tpu_custom_call" | custom-call | flops 1000000 | bytes 1609728 | tf_op jit(solution)/shard_map/pallas_call | solution.py:54
  35.7 9.0 %all-to-all-start = ((f32[8,168,128]{2,1,0:T(8,128)}), f32[8,168,128]{2,1,0:T(8,128)S(1)}, u32[]{:S(2)}, u32[]{:S(2)}) async-start(f32[8,168,128]{2,1,0:T(8,128)} %get-tuple-element.58), calls=%async_computation | async-start | bytes 1376256 | tf_op jit(solution)/shard_map/all_to_all | solution.py:514
  44.7 1.5 %collective-permute-start.10 = (f32[320,128]{1,0:T(8,128)S(1)}, f32[320,128]{1,0:T(8,128)S(1)}, u32[]{:S(2)}, u32[]{:S(2)}) collective-permute-start(f32[320,128]{1,0:T(8,128)S(1)} %get-tuple-element.54), channel_id=1, source_target_pairs={{0,16},{8,24},{16,0},{24,8},{32,48},{40,56},{48,32},{56,40},{1,17}... | collective-permute-start | bytes 491528 | tf_op jit(solution)/shard_map/ppermute | solution.py:523
  46.2 1.2 %collective-permute-start.12 = (f32[320,128]{1,0:T(8,128)S(1)}, f32[320,128]{1,0:T(8,128)S(1)}, u32[]{:S(2)}, u32[]{:S(2)}) collective-permute-start(f32[320,128]{1,0:T(8,128)S(1)} %get-tuple-element.55), channel_id=1, source_target_pairs={{0,32},{8,40},{16,48},{24,56},{32,0},{40,8},{48,16},{56,24},{1,33}... | collective-permute-start | bytes 491528 | tf_op jit(solution)/shard_map/ppermute | solution.py:523
  48.6 6.9 %collective-permute-start.9 = (f32[320,128]{1,0:T(8,128)S(1)}, f32[320,128]{1,0:T(8,128)S(1)}, u32[]{:S(2)}, u32[]{:S(2)}) collective-permute-start(f32[320,128]{1,0:T(8,128)S(1)} %get-tuple-element.53), channel_id=1, source_target_pairs={{0,8},{8,0},{16,24},{24,16},{32,40},{40,32},{48,56},{56,48},{1,9},... | collective-permute-start | bytes 491528 | tf_op jit(solution)/shard_map/ppermute | solution.py:523
  56.1 2.8 %collective-permute-start.13 = (f32[320,128]{1,0:T(8,128)S(1)}, f32[320,128]{1,0:T(8,128)S(1)}, u32[]{:S(2)}, u32[]{:S(2)}) collective-permute-start(f32[320,128]{1,0:T(8,128)S(1)} %collective-permute-done.12.refs_4_), channel_id=1, source_target_pairs={{0,8},{8,0},{16,24},{24,16},{32,40},{40,32},{48,56},{56,48},{1,9},... | collective-permute-start | bytes 491528 | tf_op jit(solution)/shard_map/ppermute | solution.py:523
  58.9 1.7 %collective-permute-start.15 = (f32[320,128]{1,0:T(8,128)S(1)}, f32[320,128]{1,0:T(8,128)S(1)}, u32[]{:S(2)}, u32[]{:S(2)}) collective-permute-start(f32[320,128]{1,0:T(8,128)S(1)} %collective-permute-done.14.refs_6_), channel_id=1, source_target_pairs={{0,8},{8,0},{16,24},{24,16},{32,40},{40,32},{48,56},{56,48},{1,9},... | collective-permute-start | bytes 491528 | tf_op jit(solution)/shard_map/ppermute | solution.py:523
  64.4 4.1 %shard_map.100.refs_0_.vy_far = f32[2560,128]{1,0:T(8,128)S(1)} custom-call(f32[2560,128]{1,0:T(8,128)S(1)} %get-tuple-element.49.v1_far, bf16[5,32,432]{2,1,0:T(8,128)(2,1)S(1)} %copy-done.9, bf16[5,128,96]{2,1,0:T(8,128)(2,1)S(1)} %get-tuple-element.51.qy.refs_10_, f32[320,128]{1,0:T(8,128)S(1)} %copy-done.11, ...), custom_call_target="tpu_custom_call" | custom-call | flops 1000000 | bytes 3046400 | tf_op jit(solution)/shard_map/pallas_call | solution.py:54
  69.8 1.5 %collective-permute-start.21 = (f32[88,128]{1,0:T(8,128)S(1)}, f32[88,128]{1,0:T(8,128)S(1)}, u32[]{:S(2)}, u32[]{:S(2)}) collective-permute-start(f32[88,128]{1,0:T(8,128)S(1)} %get-tuple-element.63.refs_0_), channel_id=1, source_target_pairs={{0,48},{8,56},{16,32},{24,40},{32,16},{40,24},{48,0},{56,8},{1,49}... | collective-permute-start | bytes 135176 | tf_op jit(solution)/shard_map/ppermute | solution.py:523
  71.9 1.3 %collective-permute-start.17 = (f32[88,128]{1,0:T(8,128)S(1)}, f32[88,128]{1,0:T(8,128)S(1)}, u32[]{:S(2)}, u32[]{:S(2)}) collective-permute-start(f32[88,128]{1,0:T(8,128)S(1)} %get-tuple-element.63.refs_0_), channel_id=1, source_target_pairs={{0,16},{8,24},{16,0},{24,8},{32,48},{40,56},{48,32},{56,40},{1,17}... | collective-permute-start | bytes 135176 | tf_op jit(solution)/shard_map/ppermute | solution.py:523
  73.2 1.2 %collective-permute-start.16 = (f32[88,128]{1,0:T(8,128)S(1)}, f32[88,128]{1,0:T(8,128)S(1)}, u32[]{:S(2)}, u32[]{:S(2)}) collective-permute-start(f32[88,128]{1,0:T(8,128)S(1)} %get-tuple-element.63.refs_0_), channel_id=1, source_target_pairs={{0,8},{8,0},{16,24},{24,16},{32,40},{40,32},{48,56},{56,48},{1,9},... | collective-permute-start | bytes 135176 | tf_op jit(solution)/shard_map/ppermute | solution.py:523
  75.7 1.8 %collective-permute-start.20 = (f32[88,128]{1,0:T(8,128)S(1)}, f32[88,128]{1,0:T(8,128)S(1)}, u32[]{:S(2)}, u32[]{:S(2)}) collective-permute-start(f32[88,128]{1,0:T(8,128)S(1)} %collective-permute-done.19.refs_4_), channel_id=1, source_target_pairs={{0,8},{8,0},{16,24},{24,16},{32,40},{40,32},{48,56},{56,48},{1,9},... | collective-permute-start | bytes 135176 | tf_op jit(solution)/shard_map/ppermute | solution.py:523
  78.8 3.0 %shard_map.103 = (f32[2560,128]{1,0:T(8,128)}, f32[5]{0:T(128)}) custom-call(f32[2560,128]{1,0:T(8,128)S(1)} %shard_map.102.v2, f32[88,128]{1,0:T(8,128)S(1)} %get-tuple-element.63.refs_0_, f32[88,128]{1,0:T(8,128)S(1)} %collective-permute-done.16.refs_1_, f32[88,128]{1,0:T(8,128)S(1)} %collective-permute-done.17.refs_2_, ...), custom_call_target="tpu_custom_call" | custom-call | flops 1000000 | bytes 1870848 | tf_op jit(solution)/shard_map/pallas_call | solution.py:54
  (79 shorter events, 14.8 us)
Async XLA Ops:
  2.7 11.2 %collective-permute-start.2 = (f32[320,128]{1,0:T(8,128)S(1)}, f32[320,128]{1,0:T(8,128)S(1)}, u32[]{:S(2)}, u32[]{:S(2)}) collective-permute-start(f32[320,128]{1,0:T(8,128)S(1)} %get-tuple-element.37), channel_id=1, source_target_pairs={{0,8},{8,16},{16,24},{24,32},{32,40},{40,48},{48,56},{56,0},{1,9},... | collective-permute-start | bytes 491528 | tf_op jit(solution)/shard_map/ppermute | solution.py:519
  4.5 9.4 %collective-permute-start.3 = (f32[320,128]{1,0:T(8,128)S(1)}, f32[320,128]{1,0:T(8,128)S(1)}, u32[]{:S(2)}, u32[]{:S(2)}) collective-permute-start(f32[320,128]{1,0:T(8,128)S(1)} %get-tuple-element.38), channel_id=1, source_target_pairs={{0,56},{8,0},{16,8},{24,16},{32,24},{40,32},{48,40},{56,48},{1,57}... | collective-permute-start | bytes 491528 | tf_op jit(solution)/shard_map/ppermute | solution.py:519
  4.5 9.3 %collective-permute-start.4 = (f32[160,128]{1,0:T(8,128)S(1)}, f32[160,128]{1,0:T(8,128)S(1)}, u32[]{:S(2)}, u32[]{:S(2)}) collective-permute-start(f32[160,128]{1,0:T(8,128)S(1)} %get-tuple-element.39), channel_id=1, source_target_pairs={{0,1},{1,2},{2,3},{3,4},{4,5},{5,6},{6,7},{7,0},{8,9},{9,10},{10,1... | collective-permute-start | bytes 245768 | tf_op jit(solution)/shard_map/ppermute | solution.py:519
  6.2 7.7 %collective-permute-start.5 = (f32[160,128]{1,0:T(8,128)S(1)}, f32[160,128]{1,0:T(8,128)S(1)}, u32[]{:S(2)}, u32[]{:S(2)}) collective-permute-start(f32[160,128]{1,0:T(8,128)S(1)} %get-tuple-element.40), channel_id=1, source_target_pairs={{0,7},{1,0},{2,1},{3,2},{4,3},{5,4},{6,5},{7,6},{8,15},{9,8},{10,9... | collective-permute-start | bytes 245768 | tf_op jit(solution)/shard_map/ppermute | solution.py:519
  6.2 2.8 %collective-permute-start = (f32[16,512]{1,0:T(8,128)S(1)}, f32[16,512]{1,0:T(8,128)S(1)}, u32[]{:S(2)}, u32[]{:S(2)}) collective-permute-start(f32[16,512]{1,0:T(8,128)S(1)} %get-tuple-element.35.own_hi), channel_id=1, source_target_pairs={{0,64},{64,128},{128,192},{192,0},{1,65},{65,129},{129,193},{193,1... | collective-permute-start | bytes 98312 | tf_op jit(solution)/shard_map/ppermute | solution.py:519
  9.0 4.9 %collective-permute-start.1 = (f32[16,512]{1,0:T(8,128)S(1)}, f32[16,512]{1,0:T(8,128)S(1)}, u32[]{:S(2)}, u32[]{:S(2)}) collective-permute-start(f32[16,512]{1,0:T(8,128)S(1)} %get-tuple-element.36.own_lo), channel_id=1, source_target_pairs={{0,192},{64,0},{128,64},{192,128},{1,193},{65,1},{129,65},{193,129... | collective-permute-start | bytes 98312 | tf_op jit(solution)/shard_map/ppermute | solution.py:519
  23.2 8.5 %collective-permute-start.8 = (f32[24,512]{1,0:T(8,128)S(1)}, f32[24,512]{1,0:T(8,128)S(1)}, u32[]{:S(2)}, u32[]{:S(2)}) collective-permute-start(f32[24,512]{1,0:T(8,128)S(1)} %get-tuple-element.44.b0), channel_id=1, source_target_pairs={{0,192},{64,0},{128,64},{192,128},{1,193},{65,1},{129,65},{193,129... | collective-permute-start | bytes 147464 | tf_op jit(solution)/shard_map/ppermute | solution.py:519
  24.8 6.9 %collective-permute-start.7 = (f32[24,512]{1,0:T(8,128)S(1)}, f32[24,512]{1,0:T(8,128)S(1)}, u32[]{:S(2)}, u32[]{:S(2)}) collective-permute-start(f32[24,512]{1,0:T(8,128)S(1)} %get-tuple-element.44.b0), channel_id=1, source_target_pairs={{0,128},{64,192},{128,0},{192,64},{1,129},{65,193},{129,1},{193,65... | collective-permute-start | bytes 147464 | tf_op jit(solution)/shard_map/ppermute | solution.py:519
  24.8 6.9 %collective-permute-start.6 = (f32[24,512]{1,0:T(8,128)S(1)}, f32[24,512]{1,0:T(8,128)S(1)}, u32[]{:S(2)}, u32[]{:S(2)}) collective-permute-start(f32[24,512]{1,0:T(8,128)S(1)} %get-tuple-element.44.b0), channel_id=1, source_target_pairs={{0,64},{64,128},{128,192},{192,0},{1,65},{65,129},{129,193},{193,1... | collective-permute-start | bytes 147464 | tf_op jit(solution)/shard_map/ppermute | solution.py:519
  35.7 32.8 %all-to-all-start = ((f32[8,168,128]{2,1,0:T(8,128)}), f32[8,168,128]{2,1,0:T(8,128)S(1)}, u32[]{:S(2)}, u32[]{:S(2)}) async-start(f32[8,168,128]{2,1,0:T(8,128)} %get-tuple-element.58), calls=%async_computation | async-start | bytes 1376256 | tf_op jit(solution)/shard_map/all_to_all | solution.py:514
  44.7 10.8 %collective-permute-start.10 = (f32[320,128]{1,0:T(8,128)S(1)}, f32[320,128]{1,0:T(8,128)S(1)}, u32[]{:S(2)}, u32[]{:S(2)}) collective-permute-start(f32[320,128]{1,0:T(8,128)S(1)} %get-tuple-element.54), channel_id=1, source_target_pairs={{0,16},{8,24},{16,0},{24,8},{32,48},{40,56},{48,32},{56,40},{1,17}... | collective-permute-start | bytes 491528 | tf_op jit(solution)/shard_map/ppermute | solution.py:523
  46.2 9.9 %collective-permute-start.12 = (f32[320,128]{1,0:T(8,128)S(1)}, f32[320,128]{1,0:T(8,128)S(1)}, u32[]{:S(2)}, u32[]{:S(2)}) collective-permute-start(f32[320,128]{1,0:T(8,128)S(1)} %get-tuple-element.55), channel_id=1, source_target_pairs={{0,32},{8,40},{16,48},{24,56},{32,0},{40,8},{48,16},{56,24},{1,33}... | collective-permute-start | bytes 491528 | tf_op jit(solution)/shard_map/ppermute | solution.py:523
  47.4 11.5 %collective-permute-start.14 = (f32[320,128]{1,0:T(8,128)S(1)}, f32[320,128]{1,0:T(8,128)S(1)}, u32[]{:S(2)}, u32[]{:S(2)}) collective-permute-start(f32[320,128]{1,0:T(8,128)S(1)} %get-tuple-element.56), channel_id=1, source_target_pairs={{0,48},{8,56},{16,32},{24,40},{32,16},{40,24},{48,0},{56,8},{1,49}... | collective-permute-start | bytes 491528 | tf_op jit(solution)/shard_map/ppermute | solution.py:523
  48.6 12.0 %collective-permute-start.9 = (f32[320,128]{1,0:T(8,128)S(1)}, f32[320,128]{1,0:T(8,128)S(1)}, u32[]{:S(2)}, u32[]{:S(2)}) collective-permute-start(f32[320,128]{1,0:T(8,128)S(1)} %get-tuple-element.53), channel_id=1, source_target_pairs={{0,8},{8,0},{16,24},{24,16},{32,40},{40,32},{48,56},{56,48},{1,9},... | collective-permute-start | bytes 491528 | tf_op jit(solution)/shard_map/ppermute | solution.py:523
  55.5 5.1 %collective-permute-start.11 = (f32[320,128]{1,0:T(8,128)S(1)}, f32[320,128]{1,0:T(8,128)S(1)}, u32[]{:S(2)}, u32[]{:S(2)}) collective-permute-start(f32[320,128]{1,0:T(8,128)S(1)} %collective-permute-done.10.refs_2_), channel_id=1, source_target_pairs={{0,8},{8,0},{16,24},{24,16},{32,40},{40,32},{48,56},{56,48},{1,9},... | collective-permute-start | bytes 491528 | tf_op jit(solution)/shard_map/ppermute | solution.py:523
  56.1 4.5 %collective-permute-start.13 = (f32[320,128]{1,0:T(8,128)S(1)}, f32[320,128]{1,0:T(8,128)S(1)}, u32[]{:S(2)}, u32[]{:S(2)}) collective-permute-start(f32[320,128]{1,0:T(8,128)S(1)} %collective-permute-done.12.refs_4_), channel_id=1, source_target_pairs={{0,8},{8,0},{16,24},{24,16},{32,40},{40,32},{48,56},{56,48},{1,9},... | collective-permute-start | bytes 491528 | tf_op jit(solution)/shard_map/ppermute | solution.py:523
  58.9 2.8 %collective-permute-start.15 = (f32[320,128]{1,0:T(8,128)S(1)}, f32[320,128]{1,0:T(8,128)S(1)}, u32[]{:S(2)}, u32[]{:S(2)}) collective-permute-start(f32[320,128]{1,0:T(8,128)S(1)} %collective-permute-done.14.refs_6_), channel_id=1, source_target_pairs={{0,8},{8,0},{16,24},{24,16},{32,40},{40,32},{48,56},{56,48},{1,9},... | collective-permute-start | bytes 491528 | tf_op jit(solution)/shard_map/ppermute | solution.py:523
  69.8 4.6 %collective-permute-start.21 = (f32[88,128]{1,0:T(8,128)S(1)}, f32[88,128]{1,0:T(8,128)S(1)}, u32[]{:S(2)}, u32[]{:S(2)}) collective-permute-start(f32[88,128]{1,0:T(8,128)S(1)} %get-tuple-element.63.refs_0_), channel_id=1, source_target_pairs={{0,48},{8,56},{16,32},{24,40},{32,16},{40,24},{48,0},{56,8},{1,49}... | collective-permute-start | bytes 135176 | tf_op jit(solution)/shard_map/ppermute | solution.py:523
  71.3 4.4 %collective-permute-start.19 = (f32[88,128]{1,0:T(8,128)S(1)}, f32[88,128]{1,0:T(8,128)S(1)}, u32[]{:S(2)}, u32[]{:S(2)}) collective-permute-start(f32[88,128]{1,0:T(8,128)S(1)} %get-tuple-element.63.refs_0_), channel_id=1, source_target_pairs={{0,32},{8,40},{16,48},{24,56},{32,0},{40,8},{48,16},{56,24},{1,33}... | collective-permute-start | bytes 135176 | tf_op jit(solution)/shard_map/ppermute | solution.py:523
  71.9 5.6 %collective-permute-start.17 = (f32[88,128]{1,0:T(8,128)S(1)}, f32[88,128]{1,0:T(8,128)S(1)}, u32[]{:S(2)}, u32[]{:S(2)}) collective-permute-start(f32[88,128]{1,0:T(8,128)S(1)} %get-tuple-element.63.refs_0_), channel_id=1, source_target_pairs={{0,16},{8,24},{16,0},{24,8},{32,48},{40,56},{48,32},{56,40},{1,17}... | collective-permute-start | bytes 135176 | tf_op jit(solution)/shard_map/ppermute | solution.py:523
  73.2 5.5 %collective-permute-start.16 = (f32[88,128]{1,0:T(8,128)S(1)}, f32[88,128]{1,0:T(8,128)S(1)}, u32[]{:S(2)}, u32[]{:S(2)}) collective-permute-start(f32[88,128]{1,0:T(8,128)S(1)} %get-tuple-element.63.refs_0_), channel_id=1, source_target_pairs={{0,8},{8,0},{16,24},{24,16},{32,40},{40,32},{48,56},{56,48},{1,9},... | collective-permute-start | bytes 135176 | tf_op jit(solution)/shard_map/ppermute | solution.py:523
  74.4 4.3 %collective-permute-start.22 = (f32[88,128]{1,0:T(8,128)S(1)}, f32[88,128]{1,0:T(8,128)S(1)}, u32[]{:S(2)}, u32[]{:S(2)}) collective-permute-start(f32[88,128]{1,0:T(8,128)S(1)} %collective-permute-done.21.refs_6_), channel_id=1, source_target_pairs={{0,8},{8,0},{16,24},{24,16},{32,40},{40,32},{48,56},{56,48},{1,9},... | collective-permute-start | bytes 135176 | tf_op jit(solution)/shard_map/ppermute | solution.py:523
  75.7 2.9 %collective-permute-start.20 = (f32[88,128]{1,0:T(8,128)S(1)}, f32[88,128]{1,0:T(8,128)S(1)}, u32[]{:S(2)}, u32[]{:S(2)}) collective-permute-start(f32[88,128]{1,0:T(8,128)S(1)} %collective-permute-done.19.refs_4_), channel_id=1, source_target_pairs={{0,8},{8,0},{16,24},{24,16},{32,40},{40,32},{48,56},{56,48},{1,9},... | collective-permute-start | bytes 135176 | tf_op jit(solution)/shard_map/ppermute | solution.py:523
  77.5 1.2 %collective-permute-start.18 = (f32[88,128]{1,0:T(8,128)S(1)}, f32[88,128]{1,0:T(8,128)S(1)}, u32[]{:S(2)}, u32[]{:S(2)}) collective-permute-start(f32[88,128]{1,0:T(8,128)S(1)} %collective-permute-done.17.refs_2_), channel_id=1, source_target_pairs={{0,8},{8,0},{16,24},{24,16},{32,40},{40,32},{48,56},{56,48},{1,9},... | collective-permute-start | bytes 135176 | tf_op jit(solution)/shard_map/ppermute | solution.py:523
  (23 other events, 92.0 us)
where the time goes:
time: 82.3 us; the launch traced here: 81.9 us
  starting transfers between devices  41.7 us (51%)
  Pallas kernels  27.2 us (33%)
  local copies, waits for them, and re-layouts  9.02 us (11%)
  waiting for transfers between devices  2.84 us (3%)
  between operations  1.13 us (1%)
    pallas_call x9, Pallas kernels, call(): pl.pallas_call(body, out_shape=[jax.ShapeDtypeStruct(*o) for o in out], i...  27.2 us
    ppermute x14, starting transfers between devices, swapped(): lax.ppermute(x, axis, [(i, i ^ k) for i in range(lax.axis_size(axis))])  23.4 us
    ppermute x9, starting transfers between devices, shifted(): return lax.ppermute(x, axis, [(i, (i + by) % size) for i in range(size)])  9.33 us
    unnamed x46, local copies, waits for them, and re-layouts  9.02 us
    all_to_all x1, starting transfers between devices, handed(): return lax.all_to_all(x, axis, 0, 0, tiled=True)  8.99 us
  transfers between devices with their start and end apart: 24, of which 4 were waited for; matrix products, arithmetic and copies ran while one was open for 0% of the time, Pallas kernels for 15%

commit v1 on v0

--- a/solution.py
+++ b/solution.py
@@ -349,7 +349,7 @@
         speed = jnp.abs(velocity[0]) + jnp.abs(velocity[1]) + jnp.abs(velocity[2])
         return jnp.maximum(top, speed + jnp.sqrt((3.0 * 1.4 * 0.4) * internal))
 
-    top = lax.fori_loop(0, 32, plane, jnp.zeros((16, 128), F32), unroll=2)
+    top = lax.fori_loop(0, 32, plane, jnp.zeros((16, 128), F32), unroll=4)
 
     lane = iota((16, 128), 1)
     edges = (lane < 2) | (lane >= 126)
@@ -392,7 +392,7 @@
 
 
 def spread_body(w, b0, b1, b2, b3, nx, qx, ty, tz, *rest):
-    far, (mine, ydown, yup), towards, (v1, zp, wide, sem) = rest[:2], rest[2:5], rest[5:9], rest[9:]
+    far, mine, towards, (v1, zp, wide, sem) = rest[:2], rest[2], rest[3:7], rest[7:]
     me, iz = lax.axis_index("gy"), lax.axis_index("gz")
     ups = [(me & 1) == 0] + [((me >> 1) ^ j) > (me >> 1) for j in (1, 2, 3)]
     blank = jnp.zeros((8, 512), F32)
@@ -419,8 +419,6 @@
         for t in range(4):
             sent = small_solve(ty[v], [v1[pl.ds(512 * v + 128 * t + y, 8, stride=16), :] for y in (0, 1, 14, 15)])
             at = 16 * (4 * v + t)
-            ydown[at : at + 16, :] = sent[0:16]
-            yup[at : at + 16, :] = sent[16:32]
             for up, out in zip(ups, towards):
                 out[at : at + 16, :] = jnp.where(up, sent[16:32], sent[0:16])
         at = pl.ds(32 * v, 32)
@@ -446,6 +444,21 @@
         for j, (h, y) in enumerate(((0, 0), (0, 1), (1, 6), (1, 7))):
             zy[pl.ds(16 * v + j, 4, stride=4), :] = zc[pl.ds(32 * (2 * v + h) + y, 4, stride=8), :]
     zy[80:88, :] = merged_stats([zr[168 * q + 160 : 168 * q + 168, :] for q in range(8)])
+
+
+def own_body(v1_far, ty, down, up, v1, sem):
+    copies = []
+    for v in range(VARS):
+        at = pl.ds(512 * v, 512)
+        copies.append(pltpu.make_async_copy(v1_far.at[at], v1.at[at], sem.at[v]))
+        copies[v].start()
+    for v in range(VARS):
+        copies[v].wait()
+        for t in range(4):
+            own = small_solve(ty[v], [v1[pl.ds(512 * v + 128 * t + y, 8, stride=16), :] for y in (0, 1, 14, 15)])
+            at = 16 * (4 * v + t)
+            down[at : at + 16, :] = own[0:16]
+            up[at : at + 16, :] = own[16:32]
 
 
 def middle_y_body(v1_far, my, qy, *refs):
@@ -565,20 +578,21 @@
         smem=(0,),
     )
     big, tall, flat = ((2560, 128), F32), ((8, 168, 128), F32), ((320, 128), F32)
-    v1, zp, mine, ydown, yup, pair, *chips = call(
+    v1, zp, mine, pair, *chips = call(
         spread_body,
-        [big, tall, ((160, 128), F32)] + [flat] * 6,
+        [big, tall, ((160, 128), F32)] + [flat] * 4,
         (w, *pieces, nx, qx, ty, tz),
         scratch=[big, tall, ((128, 512), F32)],
         far_out=(0, 1),
         sems=11,
     )
     zr = handed(zp, "gz").reshape(1344, 128)
-    lines = [ydown, swapped(pair, "gy", 1)]
+    lines = [swapped(pair, "gy", 1)]
     for j in (1, 2, 3):
         lines.append(swapped(chips[j - 1], "gy", 2 * j))
         lines.append(swapped(lines[-1], "gy", 1))
-    lines.append(yup)
+    down, up = call(own_body, [flat, flat], (v1, ty), scratch=[big], far=(0,), sems=5)
+    lines = [down, *lines, up]
     (vy,) = call(
         middle_y_body,
         [big],

time: 82.3 us -> 79.2 us (0.962)
  the two profiles are of different devices: /device:TPU:41 before, /device:TPU:1 now
where the time goes in v1:
time: 79.2 us; the launch traced here: 78.9 us
  starting transfers between devices  42.5 us (54%)
  Pallas kernels  27.3 us (34%)
  local copies, waits for them, and re-layouts  4.95 us (6%)
  waiting for transfers between devices  3.01 us (4%)
  between operations  1.17 us (1%)
    pallas_call x10, Pallas kernels, call(): pl.pallas_call(body, out_shape=[jax.ShapeDtypeStruct(*o) for o in out], i...  27.3 us
    ppermute x14, starting transfers between devices, swapped(): lax.ppermute(x, axis, [(i, i ^ k) for i in range(lax.axis_size(axis))])  24.2 us
    ppermute x9, starting transfers between devices, shifted(): return lax.ppermute(x, axis, [(i, (i + by) % size) for i in range(size)])  12.8 us
    all_to_all x1, starting transfers between devices, handed(): return lax.all_to_all(x, axis, 0, 0, tiled=True)  5.47 us
    unnamed x38, local copies, waits for them, and re-layouts  4.95 us
    ppermute x9, waiting for transfers between devices, shifted(): return lax.ppermute(x, axis, [(i, (i + by) % size) for i in range(size)])  2.88 us
  transfers between devices with their start and end apart: 24, of which 2 were waited for; matrix products, arithmetic and copies ran while one was open for 0% of the time, Pallas kernels for 17%

profile of v1, /device:TPU:1, one launch (start us, length us, event | category | flops | bytes accessed | tf_op | source)
XLA Modules:
  0.0 78.9 jit_solution(13139036854295321497)
XLA Ops:
  0.6 1.3 %copy-done = f32[5,32,16,128]{3,2,1,0:T(8,128)S(1)} copy-done((f32[5,32,16,128]{3,2,1,0:T(8,128)S(1)}, f32[5,32,16,128]{3,2,1,0:T(8,128)}, u32[]{:S(2)}) %copy-start) | copy-done | bytes 1310744
  2.7 2.6 %collective-permute-start.2 = (f32[320,128]{1,0:T(8,128)S(1)}, f32[320,128]{1,0:T(8,128)S(1)}, u32[]{:S(2)}, u32[]{:S(2)}) collective-permute-start(f32[320,128]{1,0:T(8,128)S(1)} %get-tuple-element.37), channel_id=1, source_target_pairs={{0,8},{8,16},{16,24},{24,32},{32,40},{40,48},{48,56},{56,0},{1,9},... | collective-permute-start | bytes 491528 | tf_op jit(solution)/shard_map/ppermute | solution.py:532
  7.0 3.9 %collective-permute-start.5 = (f32[160,128]{1,0:T(8,128)S(1)}, f32[160,128]{1,0:T(8,128)S(1)}, u32[]{:S(2)}, u32[]{:S(2)}) collective-permute-start(f32[160,128]{1,0:T(8,128)S(1)} %get-tuple-element.40), channel_id=1, source_target_pairs={{0,7},{1,0},{2,1},{3,2},{4,3},{5,4},{6,5},{7,6},{8,15},{9,8},{10,9... | collective-permute-start | bytes 245768 | tf_op jit(solution)/shard_map/ppermute | solution.py:532
  10.9 1.3 %collective-permute-start = (f32[16,512]{1,0:T(8,128)S(1)}, f32[16,512]{1,0:T(8,128)S(1)}, u32[]{:S(2)}, u32[]{:S(2)}) collective-permute-start(f32[16,512]{1,0:T(8,128)S(1)} %get-tuple-element.35.own_hi), channel_id=1, source_target_pairs={{0,64},{64,128},{128,192},{192,0},{1,65},{65,129},{129,193},{193,1... | collective-permute-start | bytes 98312 | tf_op jit(solution)/shard_map/ppermute | solution.py:532
  12.2 2.9 %collective-permute-done.xlo = f32[16,512]{1,0:T(8,128)S(1)} collective-permute-done((f32[16,512]{1,0:T(8,128)S(1)}, f32[16,512]{1,0:T(8,128)S(1)}, u32[]{:S(2)}, u32[]{:S(2)}) %collective-permute-start) | collective-permute-done | bytes 32800 | tf_op jit(solution)/shard_map/ppermute | solution.py:532
  15.1 1.3 %collective-permute-start.1 = (f32[16,512]{1,0:T(8,128)S(1)}, f32[16,512]{1,0:T(8,128)S(1)}, u32[]{:S(2)}, u32[]{:S(2)}) collective-permute-start(f32[16,512]{1,0:T(8,128)S(1)} %get-tuple-element.36.own_lo), channel_id=1, source_target_pairs={{0,192},{64,0},{128,64},{192,128},{1,193},{65,1},{129,65},{193,129... | collective-permute-start | bytes 98312 | tf_op jit(solution)/shard_map/ppermute | solution.py:532
  18.1 1.8 %shard_map.96 = (bf16[5,128,384]{2,1,0:T(8,128)(2,1)S(1)}, bf16[5,256,768]{2,1,0:T(8,128)(2,1)S(1)}) custom-call(f32[5,16,16]{2,1,0:T(8,128)S(1)} %copy-done.10, f32[5,32,32]{2,1,0:T(8,128)S(1)} %copy-done.5), custom_call_target="tpu_custom_call" | custom-call | flops 1000000 | bytes 25600 | tf_op jit(solution)/shard_map/pallas_call | solution.py:54
  21.0 7.5 %shard_map.97 = (f32[2560,128]{1,0:T(8,128)S(1)}, f32[24,512]{1,0:T(8,128)S(1)}, f32[32,128]{1,0:T(8,128)S(1)}) custom-call(f32[2560,128]{1,0:T(8,128)S(1)} %bitcast.4, f32[16,512]{1,0:T(8,128)S(1)} %collective-permute-done.xlo, f32[16,512]{1,0:T(8,128)S(1)} %collective-permute-done.1.xhi, f32[320,128]{1,0:T(8,128)S(1)} %collective-permute-done.2.ylo, ...), custom_call_target="tpu_custom_call" | custom-call | flops 1000000 | bytes 4718592 | tf_op jit(solution)/shard_map/pallas_call | solution.py:54
  29.0 1.5 %collective-permute-start.7 = (f32[24,512]{1,0:T(8,128)S(1)}, f32[24,512]{1,0:T(8,128)S(1)}, u32[]{:S(2)}, u32[]{:S(2)}) collective-permute-start(f32[24,512]{1,0:T(8,128)S(1)} %get-tuple-element.44.b0), channel_id=1, source_target_pairs={{0,128},{64,192},{128,0},{192,64},{1,129},{65,193},{129,1},{193,65... | collective-permute-start | bytes 147464 | tf_op jit(solution)/shard_map/ppermute | solution.py:532
  30.5 5.2 %shard_map.98 = (bf16[32,384]{1,0:T(8,128)(2,1)S(1)}, bf16[5,32,96]{2,1,0:T(8,128)(2,1)S(1)}, bf16[5,32,96]{2,1,0:T(8,128)(2,1)S(1)}, bf16[5,32,432]{2,1,0:T(8,1...) custom-call(f32[3,5]{1,0:T(4,128)S(1)} %copy-done.18, ...), custom_call_target="tpu_custom_call" | custom-call | flops 1000000 | bytes 71740 | tf_op jit(solution)/shard_map/pallas_call | solution.py:54
  35.8 2.6 %shard_map.99 = (f32[2560,128]{1,0:T(8,128)S(1)}, f32[8,168,128]{2,1,0:T(8,128)}, f32[160,128]{1,0:T(8,128)S(1)}, f32[320,128]{1,0:T(8,128)S(1)}, f32[320,128]{1...) custom-call(f32[2560,128]{1,0:T(8,128)S(1)} %get-tuple-element.43.w, ...), custom_call_target="tpu_custom_call" | custom-call | flops 1000000 | bytes 1609728 | tf_op jit(solution)/shard_map/pallas_call | solution.py:54
  38.4 5.5 %all-to-all-start = ((f32[8,168,128]{2,1,0:T(8,128)}), f32[8,168,128]{2,1,0:T(8,128)S(1)}, u32[]{:S(2)}, u32[]{:S(2)}) async-start(f32[8,168,128]{2,1,0:T(8,128)} %get-tuple-element.58), calls=%async_computation | async-start | bytes 1376256 | tf_op jit(solution)/shard_map/all_to_all | solution.py:527
  44.9 1.6 %collective-permute-start.12 = (f32[320,128]{1,0:T(8,128)S(1)}, f32[320,128]{1,0:T(8,128)S(1)}, u32[]{:S(2)}, u32[]{:S(2)}) collective-permute-start(f32[320,128]{1,0:T(8,128)S(1)} %get-tuple-element.55), channel_id=1, source_target_pairs={{0,32},{8,40},{16,48},{24,56},{32,0},{40,8},{48,16},{56,24},{1,33}... | collective-permute-start | bytes 491528 | tf_op jit(solution)/shard_map/ppermute | solution.py:536
  46.5 1.3 %collective-permute-start.14 = (f32[320,128]{1,0:T(8,128)S(1)}, f32[320,128]{1,0:T(8,128)S(1)}, u32[]{:S(2)}, u32[]{:S(2)}) collective-permute-start(f32[320,128]{1,0:T(8,128)S(1)} %get-tuple-element.56), channel_id=1, source_target_pairs={{0,48},{8,56},{16,32},{24,40},{32,16},{40,24},{48,0},{56,8},{1,49}... | collective-permute-start | bytes 491528 | tf_op jit(solution)/shard_map/ppermute | solution.py:536
  47.8 5.4 %collective-permute-start.9 = (f32[320,128]{1,0:T(8,128)S(1)}, f32[320,128]{1,0:T(8,128)S(1)}, u32[]{:S(2)}, u32[]{:S(2)}) collective-permute-start(f32[320,128]{1,0:T(8,128)S(1)} %get-tuple-element.53), channel_id=1, source_target_pairs={{0,8},{8,0},{16,24},{24,16},{32,40},{40,32},{48,56},{56,48},{1,9},... | collective-permute-start | bytes 491528 | tf_op jit(solution)/shard_map/ppermute | solution.py:536
  53.9 2.8 %collective-permute-start.13 = (f32[320,128]{1,0:T(8,128)S(1)}, f32[320,128]{1,0:T(8,128)S(1)}, u32[]{:S(2)}, u32[]{:S(2)}) collective-permute-start(f32[320,128]{1,0:T(8,128)S(1)} %collective-permute-done.12.refs_4_), channel_id=1, source_target_pairs={{0,8},{8,0},{16,24},{24,16},{32,40},{40,32},{48,56},{56,48},{1,9},... | collective-permute-start | bytes 491528 | tf_op jit(solution)/shard_map/ppermute | solution.py:536
  56.7 1.7 %collective-permute-start.15 = (f32[320,128]{1,0:T(8,128)S(1)}, f32[320,128]{1,0:T(8,128)S(1)}, u32[]{:S(2)}, u32[]{:S(2)}) collective-permute-start(f32[320,128]{1,0:T(8,128)S(1)} %collective-permute-done.14.refs_6_), channel_id=1, source_target_pairs={{0,8},{8,0},{16,24},{24,16},{32,40},{40,32},{48,56},{56,48},{1,9},... | collective-permute-start | bytes 491528 | tf_op jit(solution)/shard_map/ppermute | solution.py:536
  59.4 4.1 %shard_map.101.refs_0_.vy_far = f32[2560,128]{1,0:T(8,128)S(1)} custom-call(f32[2560,128]{1,0:T(8,128)S(1)} %get-tuple-element.49.v1_far, bf16[5,32,432]{2,1,0:T(8,128)(2,1)S(1)} %copy-done.9, bf16[5,128,96]{2,1,0:T(8,128)(2,1)S(1)} %get-tuple-element.51.qy.refs_10_, f32[320,128]{1,0:T(8,128)S(1)} %get-tuple-element.52.refs_0_, ...), custom_call_target="tpu_custom_call" | custom-call | flops 1000000 | bytes 3046400 | tf_op jit(solution)/shard_map/pallas_call | solution.py:54
  64.8 1.5 %collective-permute-start.21 = (f32[88,128]{1,0:T(8,128)S(1)}, f32[88,128]{1,0:T(8,128)S(1)}, u32[]{:S(2)}, u32[]{:S(2)}) collective-permute-start(f32[88,128]{1,0:T(8,128)S(1)} %get-tuple-element.63.refs_0_), channel_id=1, source_target_pairs={{0,48},{8,56},{16,32},{24,40},{32,16},{40,24},{48,0},{56,8},{1,49}... | collective-permute-start | bytes 135176 | tf_op jit(solution)/shard_map/ppermute | solution.py:536
  66.9 1.3 %collective-permute-start.17 = (f32[88,128]{1,0:T(8,128)S(1)}, f32[88,128]{1,0:T(8,128)S(1)}, u32[]{:S(2)}, u32[]{:S(2)}) collective-permute-start(f32[88,128]{1,0:T(8,128)S(1)} %get-tuple-element.63.refs_0_), channel_id=1, source_target_pairs={{0,16},{8,24},{16,0},{24,8},{32,48},{40,56},{48,32},{56,40},{1,17}... | collective-permute-start | bytes 135176 | tf_op jit(solution)/shard_map/ppermute | solution.py:536
  68.2 3.2 %collective-permute-start.16 = (f32[88,128]{1,0:T(8,128)S(1)}, f32[88,128]{1,0:T(8,128)S(1)}, u32[]{:S(2)}, u32[]{:S(2)}) collective-permute-start(f32[88,128]{1,0:T(8,128)S(1)} %get-tuple-element.63.refs_0_), channel_id=1, source_target_pairs={{0,8},{8,0},{16,24},{24,16},{32,40},{40,32},{48,56},{56,48},{1,9},... | collective-permute-start | bytes 135176 | tf_op jit(solution)/shard_map/ppermute | solution.py:536
  71.4 1.2 %collective-permute-start.22 = (f32[88,128]{1,0:T(8,128)S(1)}, f32[88,128]{1,0:T(8,128)S(1)}, u32[]{:S(2)}, u32[]{:S(2)}) collective-permute-start(f32[88,128]{1,0:T(8,128)S(1)} %collective-permute-done.21.refs_6_), channel_id=1, source_target_pairs={{0,8},{8,0},{16,24},{24,16},{32,40},{40,32},{48,56},{56,48},{1,9},... | collective-permute-start | bytes 135176 | tf_op jit(solution)/shard_map/ppermute | solution.py:536
  72.5 1.9 %collective-permute-start.20 = (f32[88,128]{1,0:T(8,128)S(1)}, f32[88,128]{1,0:T(8,128)S(1)}, u32[]{:S(2)}, u32[]{:S(2)}) collective-permute-start(f32[88,128]{1,0:T(8,128)S(1)} %collective-permute-done.19.refs_4_), channel_id=1, source_target_pairs={{0,8},{8,0},{16,24},{24,16},{32,40},{40,32},{48,56},{56,48},{1,9},... | collective-permute-start | bytes 135176 | tf_op jit(solution)/shard_map/ppermute | solution.py:536
  75.7 3.0 %shard_map.104 = (f32[2560,128]{1,0:T(8,128)}, f32[5]{0:T(128)}) custom-call(f32[2560,128]{1,0:T(8,128)S(1)} %shard_map.103.v2, f32[88,128]{1,0:T(8,128)S(1)} %get-tuple-element.63.refs_0_, f32[88,128]{1,0:T(8,128)S(1)} %collective-permute-done.16.refs_1_, f32[88,128]{1,0:T(8,128)S(1)} %collective-permute-done.17.refs_2_, ...), custom_call_target="tpu_custom_call" | custom-call | flops 1000000 | bytes 1870848 | tf_op jit(solution)/shard_map/pallas_call | solution.py:54
  (72 shorter events, 11.4 us)
Async XLA Ops:
  2.7 17.2 %collective-permute-start.2 = (f32[320,128]{1,0:T(8,128)S(1)}, f32[320,128]{1,0:T(8,128)S(1)}, u32[]{:S(2)}, u32[]{:S(2)}) collective-permute-start(f32[320,128]{1,0:T(8,128)S(1)} %get-tuple-element.37), channel_id=1, source_target_pairs={{0,8},{8,16},{16,24},{24,32},{32,40},{40,48},{48,56},{56,0},{1,9},... | collective-permute-start | bytes 491528 | tf_op jit(solution)/shard_map/ppermute | solution.py:532
  5.3 14.6 %collective-permute-start.3 = (f32[320,128]{1,0:T(8,128)S(1)}, f32[320,128]{1,0:T(8,128)S(1)}, u32[]{:S(2)}, u32[]{:S(2)}) collective-permute-start(f32[320,128]{1,0:T(8,128)S(1)} %get-tuple-element.38), channel_id=1, source_target_pairs={{0,56},{8,0},{16,8},{24,16},{32,24},{40,32},{48,40},{56,48},{1,57}... | collective-permute-start | bytes 491528 | tf_op jit(solution)/shard_map/ppermute | solution.py:532
  6.0 13.9 %collective-permute-start.4 = (f32[160,128]{1,0:T(8,128)S(1)}, f32[160,128]{1,0:T(8,128)S(1)}, u32[]{:S(2)}, u32[]{:S(2)}) collective-permute-start(f32[160,128]{1,0:T(8,128)S(1)} %get-tuple-element.39), channel_id=1, source_target_pairs={{0,1},{1,2},{2,3},{3,4},{4,5},{5,6},{6,7},{7,0},{8,9},{9,10},{10,1... | collective-permute-start | bytes 245768 | tf_op jit(solution)/shard_map/ppermute | solution.py:532
  7.0 13.0 %collective-permute-start.5 = (f32[160,128]{1,0:T(8,128)S(1)}, f32[160,128]{1,0:T(8,128)S(1)}, u32[]{:S(2)}, u32[]{:S(2)}) collective-permute-start(f32[160,128]{1,0:T(8,128)S(1)} %get-tuple-element.40), channel_id=1, source_target_pairs={{0,7},{1,0},{2,1},{3,2},{4,3},{5,4},{6,5},{7,6},{8,15},{9,8},{10,9... | collective-permute-start | bytes 245768 | tf_op jit(solution)/shard_map/ppermute | solution.py:532
  10.9 4.2 %collective-permute-start = (f32[16,512]{1,0:T(8,128)S(1)}, f32[16,512]{1,0:T(8,128)S(1)}, u32[]{:S(2)}, u32[]{:S(2)}) collective-permute-start(f32[16,512]{1,0:T(8,128)S(1)} %get-tuple-element.35.own_hi), channel_id=1, source_target_pairs={{0,64},{64,128},{128,192},{192,0},{1,65},{65,129},{129,193},{193,1... | collective-permute-start | bytes 98312 | tf_op jit(solution)/shard_map/ppermute | solution.py:532
  15.1 4.8 %collective-permute-start.1 = (f32[16,512]{1,0:T(8,128)S(1)}, f32[16,512]{1,0:T(8,128)S(1)}, u32[]{:S(2)}, u32[]{:S(2)}) collective-permute-start(f32[16,512]{1,0:T(8,128)S(1)} %get-tuple-element.36.own_lo), channel_id=1, source_target_pairs={{0,192},{64,0},{128,64},{192,128},{1,193},{65,1},{129,65},{193,129... | collective-permute-start | bytes 98312 | tf_op jit(solution)/shard_map/ppermute | solution.py:532
  28.5 7.3 %collective-permute-start.8 = (f32[24,512]{1,0:T(8,128)S(1)}, f32[24,512]{1,0:T(8,128)S(1)}, u32[]{:S(2)}, u32[]{:S(2)}) collective-permute-start(f32[24,512]{1,0:T(8,128)S(1)} %get-tuple-element.44.b0), channel_id=1, source_target_pairs={{0,192},{64,0},{128,64},{192,128},{1,193},{65,1},{129,65},{193,129... | collective-permute-start | bytes 147464 | tf_op jit(solution)/shard_map/ppermute | solution.py:532
  29.0 6.7 %collective-permute-start.7 = (f32[24,512]{1,0:T(8,128)S(1)}, f32[24,512]{1,0:T(8,128)S(1)}, u32[]{:S(2)}, u32[]{:S(2)}) collective-permute-start(f32[24,512]{1,0:T(8,128)S(1)} %get-tuple-element.44.b0), channel_id=1, source_target_pairs={{0,128},{64,192},{128,0},{192,64},{1,129},{65,193},{129,1},{193,65... | collective-permute-start | bytes 147464 | tf_op jit(solution)/shard_map/ppermute | solution.py:532
  30.5 5.3 %collective-permute-start.6 = (f32[24,512]{1,0:T(8,128)S(1)}, f32[24,512]{1,0:T(8,128)S(1)}, u32[]{:S(2)}, u32[]{:S(2)}) collective-permute-start(f32[24,512]{1,0:T(8,128)S(1)} %get-tuple-element.44.b0), channel_id=1, source_target_pairs={{0,64},{64,128},{128,192},{192,0},{1,65},{65,129},{129,193},{193,1... | collective-permute-start | bytes 147464 | tf_op jit(solution)/shard_map/ppermute | solution.py:532
  38.4 25.1 %all-to-all-start = ((f32[8,168,128]{2,1,0:T(8,128)}), f32[8,168,128]{2,1,0:T(8,128)S(1)}, u32[]{:S(2)}, u32[]{:S(2)}) async-start(f32[8,168,128]{2,1,0:T(8,128)} %get-tuple-element.58), calls=%async_computation | async-start | bytes 1376256 | tf_op jit(solution)/shard_map/all_to_all | solution.py:527
  43.9 9.4 %collective-permute-start.10 = (f32[320,128]{1,0:T(8,128)S(1)}, f32[320,128]{1,0:T(8,128)S(1)}, u32[]{:S(2)}, u32[]{:S(2)}) collective-permute-start(f32[320,128]{1,0:T(8,128)S(1)} %get-tuple-element.54), channel_id=1, source_target_pairs={{0,16},{8,24},{16,0},{24,8},{32,48},{40,56},{48,32},{56,40},{1,17}... | collective-permute-start | bytes 491528 | tf_op jit(solution)/shard_map/ppermute | solution.py:536
  44.9 9.0 %collective-permute-start.12 = (f32[320,128]{1,0:T(8,128)S(1)}, f32[320,128]{1,0:T(8,128)S(1)}, u32[]{:S(2)}, u32[]{:S(2)}) collective-permute-start(f32[320,128]{1,0:T(8,128)S(1)} %get-tuple-element.55), channel_id=1, source_target_pairs={{0,32},{8,40},{16,48},{24,56},{32,0},{40,8},{48,16},{56,24},{1,33}... | collective-permute-start | bytes 491528 | tf_op jit(solution)/shard_map/ppermute | solution.py:536
  46.5 10.1 %collective-permute-start.14 = (f32[320,128]{1,0:T(8,128)S(1)}, f32[320,128]{1,0:T(8,128)S(1)}, u32[]{:S(2)}, u32[]{:S(2)}) collective-permute-start(f32[320,128]{1,0:T(8,128)S(1)} %get-tuple-element.56), channel_id=1, source_target_pairs={{0,48},{8,56},{16,32},{24,40},{32,16},{40,24},{48,0},{56,8},{1,49}... | collective-permute-start | bytes 491528 | tf_op jit(solution)/shard_map/ppermute | solution.py:536
  47.8 11.5 %collective-permute-start.9 = (f32[320,128]{1,0:T(8,128)S(1)}, f32[320,128]{1,0:T(8,128)S(1)}, u32[]{:S(2)}, u32[]{:S(2)}) collective-permute-start(f32[320,128]{1,0:T(8,128)S(1)} %get-tuple-element.53), channel_id=1, source_target_pairs={{0,8},{8,0},{16,24},{24,16},{32,40},{40,32},{48,56},{56,48},{1,9},... | collective-permute-start | bytes 491528 | tf_op jit(solution)/shard_map/ppermute | solution.py:536
  53.3 6.0 %collective-permute-start.11 = (f32[320,128]{1,0:T(8,128)S(1)}, f32[320,128]{1,0:T(8,128)S(1)}, u32[]{:S(2)}, u32[]{:S(2)}) collective-permute-start(f32[320,128]{1,0:T(8,128)S(1)} %collective-permute-done.10.refs_2_), channel_id=1, source_target_pairs={{0,8},{8,0},{16,24},{24,16},{32,40},{40,32},{48,56},{56,48},{1,9},... | collective-permute-start | bytes 491528 | tf_op jit(solution)/shard_map/ppermute | solution.py:536
  53.9 5.4 %collective-permute-start.13 = (f32[320,128]{1,0:T(8,128)S(1)}, f32[320,128]{1,0:T(8,128)S(1)}, u32[]{:S(2)}, u32[]{:S(2)}) collective-permute-start(f32[320,128]{1,0:T(8,128)S(1)} %collective-permute-done.12.refs_4_), channel_id=1, source_target_pairs={{0,8},{8,0},{16,24},{24,16},{32,40},{40,32},{48,56},{56,48},{1,9},... | collective-permute-start | bytes 491528 | tf_op jit(solution)/shard_map/ppermute | solution.py:536
  56.7 2.8 %collective-permute-start.15 = (f32[320,128]{1,0:T(8,128)S(1)}, f32[320,128]{1,0:T(8,128)S(1)}, u32[]{:S(2)}, u32[]{:S(2)}) collective-permute-start(f32[320,128]{1,0:T(8,128)S(1)} %collective-permute-done.14.refs_6_), channel_id=1, source_target_pairs={{0,8},{8,0},{16,24},{24,16},{32,40},{40,32},{48,56},{56,48},{1,9},... | collective-permute-start | bytes 491528 | tf_op jit(solution)/shard_map/ppermute | solution.py:536
  64.8 6.5 %collective-permute-start.21 = (f32[88,128]{1,0:T(8,128)S(1)}, f32[88,128]{1,0:T(8,128)S(1)}, u32[]{:S(2)}, u32[]{:S(2)}) collective-permute-start(f32[88,128]{1,0:T(8,128)S(1)} %get-tuple-element.63.refs_0_), channel_id=1, source_target_pairs={{0,48},{8,56},{16,32},{24,40},{32,16},{40,24},{48,0},{56,8},{1,49}... | collective-permute-start | bytes 135176 | tf_op jit(solution)/shard_map/ppermute | solution.py:536
  66.3 6.2 %collective-permute-start.19 = (f32[88,128]{1,0:T(8,128)S(1)}, f32[88,128]{1,0:T(8,128)S(1)}, u32[]{:S(2)}, u32[]{:S(2)}) collective-permute-start(f32[88,128]{1,0:T(8,128)S(1)} %get-tuple-element.63.refs_0_), channel_id=1, source_target_pairs={{0,32},{8,40},{16,48},{24,56},{32,0},{40,8},{48,16},{56,24},{1,33}... | collective-permute-start | bytes 135176 | tf_op jit(solution)/shard_map/ppermute | solution.py:536
  66.9 7.5 %collective-permute-start.17 = (f32[88,128]{1,0:T(8,128)S(1)}, f32[88,128]{1,0:T(8,128)S(1)}, u32[]{:S(2)}, u32[]{:S(2)}) collective-permute-start(f32[88,128]{1,0:T(8,128)S(1)} %get-tuple-element.63.refs_0_), channel_id=1, source_target_pairs={{0,16},{8,24},{16,0},{24,8},{32,48},{40,56},{48,32},{56,40},{1,17}... | collective-permute-start | bytes 135176 | tf_op jit(solution)/shard_map/ppermute | solution.py:536
  68.2 7.5 %collective-permute-start.16 = (f32[88,128]{1,0:T(8,128)S(1)}, f32[88,128]{1,0:T(8,128)S(1)}, u32[]{:S(2)}, u32[]{:S(2)}) collective-permute-start(f32[88,128]{1,0:T(8,128)S(1)} %get-tuple-element.63.refs_0_), channel_id=1, source_target_pairs={{0,8},{8,0},{16,24},{24,16},{32,40},{40,32},{48,56},{56,48},{1,9},... | collective-permute-start | bytes 135176 | tf_op jit(solution)/shard_map/ppermute | solution.py:536
  71.4 4.3 %collective-permute-start.22 = (f32[88,128]{1,0:T(8,128)S(1)}, f32[88,128]{1,0:T(8,128)S(1)}, u32[]{:S(2)}, u32[]{:S(2)}) collective-permute-start(f32[88,128]{1,0:T(8,128)S(1)} %collective-permute-done.21.refs_6_), channel_id=1, source_target_pairs={{0,8},{8,0},{16,24},{24,16},{32,40},{40,32},{48,56},{56,48},{1,9},... | collective-permute-start | bytes 135176 | tf_op jit(solution)/shard_map/ppermute | solution.py:536
  72.5 3.2 %collective-permute-start.20 = (f32[88,128]{1,0:T(8,128)S(1)}, f32[88,128]{1,0:T(8,128)S(1)}, u32[]{:S(2)}, u32[]{:S(2)}) collective-permute-start(f32[88,128]{1,0:T(8,128)S(1)} %collective-permute-done.19.refs_4_), channel_id=1, source_target_pairs={{0,8},{8,0},{16,24},{24,16},{32,40},{40,32},{48,56},{56,48},{1,9},... | collective-permute-start | bytes 135176 | tf_op jit(solution)/shard_map/ppermute | solution.py:536
  74.5 1.2 %collective-permute-start.18 = (f32[88,128]{1,0:T(8,128)S(1)}, f32[88,128]{1,0:T(8,128)S(1)}, u32[]{:S(2)}, u32[]{:S(2)}) collective-permute-start(f32[88,128]{1,0:T(8,128)S(1)} %collective-permute-done.17.refs_2_), channel_id=1, source_target_pairs={{0,8},{8,0},{16,24},{24,16},{32,40},{40,32},{48,56},{56,48},{1,9},... | collective-permute-start | bytes 135176 | tf_op jit(solution)/shard_map/ppermute | solution.py:536
  (19 other events, 103.4 us)

commit v2 on v1

--- a/solution.py
+++ b/solution.py
@@ -391,10 +391,9 @@
     bx[20:21, :] = stats_row((1, 512), [jnp.sum(s) for s in sums], jnp.max(top))
 
 
-def spread_body(w, b0, b1, b2, b3, nx, qx, ty, tz, *rest):
-    far, mine, towards, (v1, zp, wide, sem) = rest[:2], rest[2], rest[3:7], rest[7:]
-    me, iz = lax.axis_index("gy"), lax.axis_index("gz")
-    ups = [(me & 1) == 0] + [((me >> 1) ^ j) > (me >> 1) for j in (1, 2, 3)]
+def spread_body(w, b0, b1, b2, b3, nx, qx, tz, *rest):
+    far, mine, (v1, zp, wide, sem) = rest[:2], rest[2], rest[3:]
+    iz = lax.axis_index("gz")
     blank = jnp.zeros((8, 512), F32)
     pieces = [b0, b1, b2, b3]
     data = jnp.concatenate([t for p in pieces for t in (p[...], blank)], axis=0)
@@ -416,11 +415,6 @@
             mine[at : at + 16, :] = sent[16:32]
             for p in range(8):
                 zp[p, at : at + 16, :] = jnp.where(p <= iz, sent[0:16], sent[16:32])
-        for t in range(4):
-            sent = small_solve(ty[v], [v1[pl.ds(512 * v + 128 * t + y, 8, stride=16), :] for y in (0, 1, 14, 15)])
-            at = 16 * (4 * v + t)
-            for up, out in zip(ups, towards):
-                out[at : at + 16, :] = jnp.where(up, sent[16:32], sent[0:16])
         at = pl.ds(32 * v, 32)
         copies.append(pltpu.make_async_copy(zp.at[:, at], far[1].at[:, at], sem.at[5 + v]))
         copies[-1].start()
@@ -446,7 +440,10 @@
     zy[80:88, :] = merged_stats([zr[168 * q + 160 : 168 * q + 168, :] for q in range(8)])
 
 
-def own_body(v1_far, ty, down, up, v1, sem):
+def send_y_body(v1_far, ty, down, up, *rest):
+    towards, (v1, sem) = rest[:4], rest[4:]
+    me = lax.axis_index("gy")
+    ups = [(me & 1) == 0] + [((me >> 1) ^ j) > (me >> 1) for j in (1, 2, 3)]
     copies = []
     for v in range(VARS):
         at = pl.ds(512 * v, 512)
@@ -455,10 +452,12 @@
     for v in range(VARS):
         copies[v].wait()
         for t in range(4):
-            own = small_solve(ty[v], [v1[pl.ds(512 * v + 128 * t + y, 8, stride=16), :] for y in (0, 1, 14, 15)])
+            sent = small_solve(ty[v], [v1[pl.ds(512 * v + 128 * t + y, 8, stride=16), :] for y in (0, 1, 14, 15)])
             at = 16 * (4 * v + t)
-            down[at : at + 16, :] = own[0:16]
-            up[at : at + 16, :] = own[16:32]
+            down[at : at + 16, :] = sent[0:16]
+            up[at : at + 16, :] = sent[16:32]
+            for choice, out in zip(ups, towards):
+                out[at : at + 16, :] = jnp.where(choice, sent[16:32], sent[0:16])
 
 
 def middle_y_body(v1_far, my, qy, *refs):
@@ -578,20 +577,20 @@
         smem=(0,),
     )
     big, tall, flat = ((2560, 128), F32), ((8, 168, 128), F32), ((320, 128), F32)
-    v1, zp, mine, pair, *chips = call(
+    v1, zp, mine = call(
         spread_body,
-        [big, tall, ((160, 128), F32)] + [flat] * 4,
-        (w, *pieces, nx, qx, ty, tz),
+        [big, tall, ((160, 128), F32)],
+        (w, *pieces, nx, qx, tz),
         scratch=[big, tall, ((128, 512), F32)],
         far_out=(0, 1),
         sems=11,
     )
     zr = handed(zp, "gz").reshape(1344, 128)
+    down, up, pair, *chips = call(send_y_body, [flat] * 6, (v1, ty), scratch=[big], far=(0,), sems=5)
     lines = [swapped(pair, "gy", 1)]
     for j in (1, 2, 3):
         lines.append(swapped(chips[j - 1], "gy", 2 * j))
         lines.append(swapped(lines[-1], "gy", 1))
-    down, up = call(own_body, [flat, flat], (v1, ty), scratch=[big], far=(0,), sems=5)
     lines = [down, *lines, up]
     (vy,) = call(
         middle_y_body,

time: 79.2 us -> 79.1 us (level)
  starting transfers between devices: 42.5 us -> 41.5 us
  waiting for transfers between devices: 3.01 us -> 3.93 us
    ppermute x14, starting transfers between devices: 24.2 us -> 23.3 us  [swapped(): lax.ppermute(x, axis, [(i, i ^ k) for i in range(lax.axis_size(axis))])]
    ppermute x14, waiting for transfers between devices: 0.13 us -> 1.05 us  [swapped(): lax.ppermute(x, axis, [(i, i ^ k) for i in range(lax.axis_size(axis))])]
where the time goes in v2:
time: 79.1 us; the launch traced here: 78.7 us
  starting transfers between devices  41.5 us (52%)
  Pallas kernels  27.1 us (34%)
  local copies, waits for them, and re-layouts  4.95 us (6%)
  waiting for transfers between devices  3.93 us (5%)
  between operations  1.15 us (1%)
    pallas_call x10, Pallas kernels, call(): pl.pallas_call(body, out_shape=[jax.ShapeDtypeStruct(*o) for o in out], i...  27.1 us
    ppermute x14, starting transfers between devices, swapped(): lax.ppermute(x, axis, [(i, i ^ k) for i in range(lax.axis_size(axis))])  23.3 us
    ppermute x9, starting transfers between devices, shifted(): return lax.ppermute(x, axis, [(i, (i + by) % size) for i in range(size)])  12.8 us
    all_to_all x1, starting transfers between devices, handed(): return lax.all_to_all(x, axis, 0, 0, tiled=True)  5.47 us
    unnamed x38, local copies, waits for them, and re-layouts  4.95 us
    ppermute x9, waiting for transfers between devices, shifted(): return lax.ppermute(x, axis, [(i, (i + by) % size) for i in range(size)])  2.88 us
  transfers between devices with their start and end apart: 24, of which 2 were waited for; matrix products, arithmetic and copies ran while one was open for 0% of the time, Pallas kernels for 17%

profile of v2, /device:TPU:1, one launch (start us, length us, event | category | flops | bytes accessed | tf_op | source)
XLA Modules:
  0.0 78.7 jit_solution(5731816974956315826)
XLA Ops:
  0.6 1.3 %copy-done = f32[5,32,16,128]{3,2,1,0:T(8,128)S(1)} copy-done((f32[5,32,16,128]{3,2,1,0:T(8,128)S(1)}, f32[5,32,16,128]{3,2,1,0:T(8,128)}, u32[]{:S(2)}) %copy-start) | copy-done | bytes 1310744
  2.7 2.6 %collective-permute-start.2 = (f32[320,128]{1,0:T(8,128)S(1)}, f32[320,128]{1,0:T(8,128)S(1)}, u32[]{:S(2)}, u32[]{:S(2)}) collective-permute-start(f32[320,128]{1,0:T(8,128)S(1)} %get-tuple-element.37), channel_id=1, source_target_pairs={{0,8},{8,16},{16,24},{24,32},{32,40},{40,48},{48,56},{56,0},{1,9},... | collective-permute-start | bytes 491528 | tf_op jit(solution)/shard_map/ppermute | solution.py:531
  7.0 3.9 %collective-permute-start.5 = (f32[160,128]{1,0:T(8,128)S(1)}, f32[160,128]{1,0:T(8,128)S(1)}, u32[]{:S(2)}, u32[]{:S(2)}) collective-permute-start(f32[160,128]{1,0:T(8,128)S(1)} %get-tuple-element.40), channel_id=1, source_target_pairs={{0,7},{1,0},{2,1},{3,2},{4,3},{5,4},{6,5},{7,6},{8,15},{9,8},{10,9... | collective-permute-start | bytes 245768 | tf_op jit(solution)/shard_map/ppermute | solution.py:531
  10.9 1.3 %collective-permute-start = (f32[16,512]{1,0:T(8,128)S(1)}, f32[16,512]{1,0:T(8,128)S(1)}, u32[]{:S(2)}, u32[]{:S(2)}) collective-permute-start(f32[16,512]{1,0:T(8,128)S(1)} %get-tuple-element.35.own_hi), channel_id=1, source_target_pairs={{0,64},{64,128},{128,192},{192,0},{1,65},{65,129},{129,193},{193,1... | collective-permute-start | bytes 98312 | tf_op jit(solution)/shard_map/ppermute | solution.py:531
  12.2 2.9 %collective-permute-done.xlo = f32[16,512]{1,0:T(8,128)S(1)} collective-permute-done((f32[16,512]{1,0:T(8,128)S(1)}, f32[16,512]{1,0:T(8,128)S(1)}, u32[]{:S(2)}, u32[]{:S(2)}) %collective-permute-start) | collective-permute-done | bytes 32800 | tf_op jit(solution)/shard_map/ppermute | solution.py:531
  15.1 1.3 %collective-permute-start.1 = (f32[16,512]{1,0:T(8,128)S(1)}, f32[16,512]{1,0:T(8,128)S(1)}, u32[]{:S(2)}, u32[]{:S(2)}) collective-permute-start(f32[16,512]{1,0:T(8,128)S(1)} %get-tuple-element.36.own_lo), channel_id=1, source_target_pairs={{0,192},{64,0},{128,64},{192,128},{1,193},{65,1},{129,65},{193,129... | collective-permute-start | bytes 98312 | tf_op jit(solution)/shard_map/ppermute | solution.py:531
  18.1 1.8 %shard_map.96 = (bf16[5,128,384]{2,1,0:T(8,128)(2,1)S(1)}, bf16[5,256,768]{2,1,0:T(8,128)(2,1)S(1)}) custom-call(f32[5,16,16]{2,1,0:T(8,128)S(1)} %copy-done.10, f32[5,32,32]{2,1,0:T(8,128)S(1)} %copy-done.5), custom_call_target="tpu_custom_call" | custom-call | flops 1000000 | bytes 25600 | tf_op jit(solution)/shard_map/pallas_call | solution.py:54
  21.0 7.5 %shard_map.97 = (f32[2560,128]{1,0:T(8,128)S(1)}, f32[24,512]{1,0:T(8,128)S(1)}, f32[32,128]{1,0:T(8,128)S(1)}) custom-call(f32[2560,128]{1,0:T(8,128)S(1)} %bitcast.4, f32[16,512]{1,0:T(8,128)S(1)} %collective-permute-done.xlo, f32[16,512]{1,0:T(8,128)S(1)} %collective-permute-done.1.xhi, f32[320,128]{1,0:T(8,128)S(1)} %collective-permute-done.2.ylo, ...), custom_call_target="tpu_custom_call" | custom-call | flops 1000000 | bytes 4718592 | tf_op jit(solution)/shard_map/pallas_call | solution.py:54
  29.0 1.5 %collective-permute-start.7 = (f32[24,512]{1,0:T(8,128)S(1)}, f32[24,512]{1,0:T(8,128)S(1)}, u32[]{:S(2)}, u32[]{:S(2)}) collective-permute-start(f32[24,512]{1,0:T(8,128)S(1)} %get-tuple-element.44.b0), channel_id=1, source_target_pairs={{0,128},{64,192},{128,0},{192,64},{1,129},{65,193},{129,1},{193,65... | collective-permute-start | bytes 147464 | tf_op jit(solution)/shard_map/ppermute | solution.py:531
  30.5 5.2 %shard_map.98 = (bf16[32,384]{1,0:T(8,128)(2,1)S(1)}, bf16[5,32,96]{2,1,0:T(8,128)(2,1)S(1)}, bf16[5,32,96]{2,1,0:T(8,128)(2,1)S(1)}, bf16[5,32,432]{2,1,0:T(8,1...) custom-call(f32[3,5]{1,0:T(4,128)S(1)} %copy-done.18, ...), custom_call_target="tpu_custom_call" | custom-call | flops 1000000 | bytes 71740 | tf_op jit(solution)/shard_map/pallas_call | solution.py:54
  35.8 2.4 %shard_map.99 = (f32[2560,128]{1,0:T(8,128)S(1)}, f32[8,168,128]{2,1,0:T(8,128)}, f32[160,128]{1,0:T(8,128)S(1)}) custom-call(f32[2560,128]{1,0:T(8,128)S(1)} %get-tuple-element.43.w, f32[24,512]{1,0:T(8,128)S(1)} %get-tuple-element.44.b0, f32[24,512]{1,0:T(8,128)S(1)} %collective-permute-done.6.b1, f32[24,512]{1,0:T(8,128)S(1)} %collective-permute-done.7.b2, ...), custom_call_target="tpu_custom_call" | custom-call | flops 1000000 | bytes 1579008 | tf_op jit(solution)/shard_map/pallas_call | solution.py:54
  38.2 5.5 %all-to-all-start = ((f32[8,168,128]{2,1,0:T(8,128)}), f32[8,168,128]{2,1,0:T(8,128)S(1)}, u32[]{:S(2)}, u32[]{:S(2)}) async-start(f32[8,168,128]{2,1,0:T(8,128)} %get-tuple-element.58), calls=%async_computation | async-start | bytes 1376256 | tf_op jit(solution)/shard_map/all_to_all | solution.py:526
  45.6 1.6 %collective-permute-start.12 = (f32[320,128]{1,0:T(8,128)S(1)}, f32[320,128]{1,0:T(8,128)S(1)}, u32[]{:S(2)}, u32[]{:S(2)}) collective-permute-start(f32[320,128]{1,0:T(8,128)S(1)} %get-tuple-element.55), channel_id=1, source_target_pairs={{0,32},{8,40},{16,48},{24,56},{32,0},{40,8},{48,16},{56,24},{1,33}... | collective-permute-start | bytes 491528 | tf_op jit(solution)/shard_map/ppermute | solution.py:535
  47.3 1.3 %collective-permute-start.14 = (f32[320,128]{1,0:T(8,128)S(1)}, f32[320,128]{1,0:T(8,128)S(1)}, u32[]{:S(2)}, u32[]{:S(2)}) collective-permute-start(f32[320,128]{1,0:T(8,128)S(1)} %get-tuple-element.56), channel_id=1, source_target_pairs={{0,48},{8,56},{16,32},{24,40},{32,16},{40,24},{48,0},{56,8},{1,49}... | collective-permute-start | bytes 491528 | tf_op jit(solution)/shard_map/ppermute | solution.py:535
  48.6 5.4 %collective-permute-start.9 = (f32[320,128]{1,0:T(8,128)S(1)}, f32[320,128]{1,0:T(8,128)S(1)}, u32[]{:S(2)}, u32[]{:S(2)}) collective-permute-start(f32[320,128]{1,0:T(8,128)S(1)} %get-tuple-element.53), channel_id=1, source_target_pairs={{0,8},{8,0},{16,24},{24,16},{32,40},{40,32},{48,56},{56,48},{1,9},... | collective-permute-start | bytes 491528 | tf_op jit(solution)/shard_map/ppermute | solution.py:535
  54.6 2.8 %collective-permute-start.13 = (f32[320,128]{1,0:T(8,128)S(1)}, f32[320,128]{1,0:T(8,128)S(1)}, u32[]{:S(2)}, u32[]{:S(2)}) collective-permute-start(f32[320,128]{1,0:T(8,128)S(1)} %collective-permute-done.12.refs_4_), channel_id=1, source_target_pairs={{0,8},{8,0},{16,24},{24,16},{32,40},{40,32},{48,56},{56,48},{1,9},... | collective-permute-start | bytes 491528 | tf_op jit(solution)/shard_map/ppermute | solution.py:535
  57.4 1.7 %collective-permute-start.15 = (f32[320,128]{1,0:T(8,128)S(1)}, f32[320,128]{1,0:T(8,128)S(1)}, u32[]{:S(2)}, u32[]{:S(2)}) collective-permute-start(f32[320,128]{1,0:T(8,128)S(1)} %collective-permute-done.14.refs_6_), channel_id=1, source_target_pairs={{0,8},{8,0},{16,24},{24,16},{32,40},{40,32},{48,56},{56,48},{1,9},... | collective-permute-start | bytes 491528 | tf_op jit(solution)/shard_map/ppermute | solution.py:535
  60.2 4.1 %shard_map.101.refs_0_.vy_far = f32[2560,128]{1,0:T(8,128)S(1)} custom-call(f32[2560,128]{1,0:T(8,128)S(1)} %get-tuple-element.48.v1_far, bf16[5,32,432]{2,1,0:T(8,128)(2,1)S(1)} %copy-done.9, bf16[5,128,96]{2,1,0:T(8,128)(2,1)S(1)} %get-tuple-element.50.qy.refs_10_, f32[320,128]{1,0:T(8,128)S(1)} %get-tuple-element.52.refs_0_, ...), custom_call_target="tpu_custom_call" | custom-call | flops 1000000 | bytes 3046400 | tf_op jit(solution)/shard_map/pallas_call | solution.py:54
  65.6 1.5 %collective-permute-start.21 = (f32[88,128]{1,0:T(8,128)S(1)}, f32[88,128]{1,0:T(8,128)S(1)}, u32[]{:S(2)}, u32[]{:S(2)}) collective-permute-start(f32[88,128]{1,0:T(8,128)S(1)} %get-tuple-element.63.refs_0_), channel_id=1, source_target_pairs={{0,48},{8,56},{16,32},{24,40},{32,16},{40,24},{48,0},{56,8},{1,49}... | collective-permute-start | bytes 135176 | tf_op jit(solution)/shard_map/ppermute | solution.py:535
  67.7 1.3 %collective-permute-start.17 = (f32[88,128]{1,0:T(8,128)S(1)}, f32[88,128]{1,0:T(8,128)S(1)}, u32[]{:S(2)}, u32[]{:S(2)}) collective-permute-start(f32[88,128]{1,0:T(8,128)S(1)} %get-tuple-element.63.refs_0_), channel_id=1, source_target_pairs={{0,16},{8,24},{16,0},{24,8},{32,48},{40,56},{48,32},{56,40},{1,17}... | collective-permute-start | bytes 135176 | tf_op jit(solution)/shard_map/ppermute | solution.py:535
  68.9 2.2 %collective-permute-start.16 = (f32[88,128]{1,0:T(8,128)S(1)}, f32[88,128]{1,0:T(8,128)S(1)}, u32[]{:S(2)}, u32[]{:S(2)}) collective-permute-start(f32[88,128]{1,0:T(8,128)S(1)} %get-tuple-element.63.refs_0_), channel_id=1, source_target_pairs={{0,8},{8,0},{16,24},{24,16},{32,40},{40,32},{48,56},{56,48},{1,9},... | collective-permute-start | bytes 135176 | tf_op jit(solution)/shard_map/ppermute | solution.py:535
  71.2 1.5 %collective-permute-start.22 = (f32[88,128]{1,0:T(8,128)S(1)}, f32[88,128]{1,0:T(8,128)S(1)}, u32[]{:S(2)}, u32[]{:S(2)}) collective-permute-start(f32[88,128]{1,0:T(8,128)S(1)} %collective-permute-done.21.refs_6_), channel_id=1, source_target_pairs={{0,8},{8,0},{16,24},{24,16},{32,40},{40,32},{48,56},{56,48},{1,9},... | collective-permute-start | bytes 135176 | tf_op jit(solution)/shard_map/ppermute | solution.py:535
  72.7 1.6 %collective-permute-start.20 = (f32[88,128]{1,0:T(8,128)S(1)}, f32[88,128]{1,0:T(8,128)S(1)}, u32[]{:S(2)}, u32[]{:S(2)}) collective-permute-start(f32[88,128]{1,0:T(8,128)S(1)} %collective-permute-done.19.refs_4_), channel_id=1, source_target_pairs={{0,8},{8,0},{16,24},{24,16},{32,40},{40,32},{48,56},{56,48},{1,9},... | collective-permute-start | bytes 135176 | tf_op jit(solution)/shard_map/ppermute | solution.py:535
  75.5 3.0 %shard_map.104 = (f32[2560,128]{1,0:T(8,128)}, f32[5]{0:T(128)}) custom-call(f32[2560,128]{1,0:T(8,128)S(1)} %shard_map.103.v2, f32[88,128]{1,0:T(8,128)S(1)} %get-tuple-element.63.refs_0_, f32[88,128]{1,0:T(8,128)S(1)} %collective-permute-done.16.refs_1_, f32[88,128]{1,0:T(8,128)S(1)} %collective-permute-done.17.refs_2_, ...), custom_call_target="tpu_custom_call" | custom-call | flops 1000000 | bytes 1870848 | tf_op jit(solution)/shard_map/pallas_call | solution.py:54
  (72 shorter events, 12.3 us)
Async XLA Ops:
  2.7 17.2 %collective-permute-start.2 = (f32[320,128]{1,0:T(8,128)S(1)}, f32[320,128]{1,0:T(8,128)S(1)}, u32[]{:S(2)}, u32[]{:S(2)}) collective-permute-start(f32[320,128]{1,0:T(8,128)S(1)} %get-tuple-element.37), channel_id=1, source_target_pairs={{0,8},{8,16},{16,24},{24,32},{32,40},{40,48},{48,56},{56,0},{1,9},... | collective-permute-start | bytes 491528 | tf_op jit(solution)/shard_map/ppermute | solution.py:531
  5.3 14.6 %collective-permute-start.3 = (f32[320,128]{1,0:T(8,128)S(1)}, f32[320,128]{1,0:T(8,128)S(1)}, u32[]{:S(2)}, u32[]{:S(2)}) collective-permute-start(f32[320,128]{1,0:T(8,128)S(1)} %get-tuple-element.38), channel_id=1, source_target_pairs={{0,56},{8,0},{16,8},{24,16},{32,24},{40,32},{48,40},{56,48},{1,57}... | collective-permute-start | bytes 491528 | tf_op jit(solution)/shard_map/ppermute | solution.py:531
  6.0 13.9 %collective-permute-start.4 = (f32[160,128]{1,0:T(8,128)S(1)}, f32[160,128]{1,0:T(8,128)S(1)}, u32[]{:S(2)}, u32[]{:S(2)}) collective-permute-start(f32[160,128]{1,0:T(8,128)S(1)} %get-tuple-element.39), channel_id=1, source_target_pairs={{0,1},{1,2},{2,3},{3,4},{4,5},{5,6},{6,7},{7,0},{8,9},{9,10},{10,1... | collective-permute-start | bytes 245768 | tf_op jit(solution)/shard_map/ppermute | solution.py:531
  7.0 13.0 %collective-permute-start.5 = (f32[160,128]{1,0:T(8,128)S(1)}, f32[160,128]{1,0:T(8,128)S(1)}, u32[]{:S(2)}, u32[]{:S(2)}) collective-permute-start(f32[160,128]{1,0:T(8,128)S(1)} %get-tuple-element.40), channel_id=1, source_target_pairs={{0,7},{1,0},{2,1},{3,2},{4,3},{5,4},{6,5},{7,6},{8,15},{9,8},{10,9... | collective-permute-start | bytes 245768 | tf_op jit(solution)/shard_map/ppermute | solution.py:531
  10.9 4.2 %collective-permute-start = (f32[16,512]{1,0:T(8,128)S(1)}, f32[16,512]{1,0:T(8,128)S(1)}, u32[]{:S(2)}, u32[]{:S(2)}) collective-permute-start(f32[16,512]{1,0:T(8,128)S(1)} %get-tuple-element.35.own_hi), channel_id=1, source_target_pairs={{0,64},{64,128},{128,192},{192,0},{1,65},{65,129},{129,193},{193,1... | collective-permute-start | bytes 98312 | tf_op jit(solution)/shard_map/ppermute | solution.py:531
  15.1 4.8 %collective-permute-start.1 = (f32[16,512]{1,0:T(8,128)S(1)}, f32[16,512]{1,0:T(8,128)S(1)}, u32[]{:S(2)}, u32[]{:S(2)}) collective-permute-start(f32[16,512]{1,0:T(8,128)S(1)} %get-tuple-element.36.own_lo), channel_id=1, source_target_pairs={{0,192},{64,0},{128,64},{192,128},{1,193},{65,1},{129,65},{193,129... | collective-permute-start | bytes 98312 | tf_op jit(solution)/shard_map/ppermute | solution.py:531
  28.5 7.3 %collective-permute-start.8 = (f32[24,512]{1,0:T(8,128)S(1)}, f32[24,512]{1,0:T(8,128)S(1)}, u32[]{:S(2)}, u32[]{:S(2)}) collective-permute-start(f32[24,512]{1,0:T(8,128)S(1)} %get-tuple-element.44.b0), channel_id=1, source_target_pairs={{0,192},{64,0},{128,64},{192,128},{1,193},{65,1},{129,65},{193,129... | collective-permute-start | bytes 147464 | tf_op jit(solution)/shard_map/ppermute | solution.py:531
  29.0 6.7 %collective-permute-start.7 = (f32[24,512]{1,0:T(8,128)S(1)}, f32[24,512]{1,0:T(8,128)S(1)}, u32[]{:S(2)}, u32[]{:S(2)}) collective-permute-start(f32[24,512]{1,0:T(8,128)S(1)} %get-tuple-element.44.b0), channel_id=1, source_target_pairs={{0,128},{64,192},{128,0},{192,64},{1,129},{65,193},{129,1},{193,65... | collective-permute-start | bytes 147464 | tf_op jit(solution)/shard_map/ppermute | solution.py:531
  30.5 5.3 %collective-permute-start.6 = (f32[24,512]{1,0:T(8,128)S(1)}, f32[24,512]{1,0:T(8,128)S(1)}, u32[]{:S(2)}, u32[]{:S(2)}) collective-permute-start(f32[24,512]{1,0:T(8,128)S(1)} %get-tuple-element.44.b0), channel_id=1, source_target_pairs={{0,64},{64,128},{128,192},{192,0},{1,65},{65,129},{129,193},{193,1... | collective-permute-start | bytes 147464 | tf_op jit(solution)/shard_map/ppermute | solution.py:531
  38.2 26.0 %all-to-all-start = ((f32[8,168,128]{2,1,0:T(8,128)}), f32[8,168,128]{2,1,0:T(8,128)S(1)}, u32[]{:S(2)}, u32[]{:S(2)}) async-start(f32[8,168,128]{2,1,0:T(8,128)} %get-tuple-element.58), calls=%async_computation | async-start | bytes 1376256 | tf_op jit(solution)/shard_map/all_to_all | solution.py:526
  44.6 9.4 %collective-permute-start.10 = (f32[320,128]{1,0:T(8,128)S(1)}, f32[320,128]{1,0:T(8,128)S(1)}, u32[]{:S(2)}, u32[]{:S(2)}) collective-permute-start(f32[320,128]{1,0:T(8,128)S(1)} %get-tuple-element.54), channel_id=1, source_target_pairs={{0,16},{8,24},{16,0},{24,8},{32,48},{40,56},{48,32},{56,40},{1,17}... | collective-permute-start | bytes 491528 | tf_op jit(solution)/shard_map/ppermute | solution.py:535
  45.6 9.0 %collective-permute-start.12 = (f32[320,128]{1,0:T(8,128)S(1)}, f32[320,128]{1,0:T(8,128)S(1)}, u32[]{:S(2)}, u32[]{:S(2)}) collective-permute-start(f32[320,128]{1,0:T(8,128)S(1)} %get-tuple-element.55), channel_id=1, source_target_pairs={{0,32},{8,40},{16,48},{24,56},{32,0},{40,8},{48,16},{56,24},{1,33}... | collective-permute-start | bytes 491528 | tf_op jit(solution)/shard_map/ppermute | solution.py:535
  47.3 10.1 %collective-permute-start.14 = (f32[320,128]{1,0:T(8,128)S(1)}, f32[320,128]{1,0:T(8,128)S(1)}, u32[]{:S(2)}, u32[]{:S(2)}) collective-permute-start(f32[320,128]{1,0:T(8,128)S(1)} %get-tuple-element.56), channel_id=1, source_target_pairs={{0,48},{8,56},{16,32},{24,40},{32,16},{40,24},{48,0},{56,8},{1,49}... | collective-permute-start | bytes 491528 | tf_op jit(solution)/shard_map/ppermute | solution.py:535
  48.6 10.6 %collective-permute-start.9 = (f32[320,128]{1,0:T(8,128)S(1)}, f32[320,128]{1,0:T(8,128)S(1)}, u32[]{:S(2)}, u32[]{:S(2)}) collective-permute-start(f32[320,128]{1,0:T(8,128)S(1)} %get-tuple-element.53), channel_id=1, source_target_pairs={{0,8},{8,0},{16,24},{24,16},{32,40},{40,32},{48,56},{56,48},{1,9},... | collective-permute-start | bytes 491528 | tf_op jit(solution)/shard_map/ppermute | solution.py:535
  54.0 5.1 %collective-permute-start.11 = (f32[320,128]{1,0:T(8,128)S(1)}, f32[320,128]{1,0:T(8,128)S(1)}, u32[]{:S(2)}, u32[]{:S(2)}) collective-permute-start(f32[320,128]{1,0:T(8,128)S(1)} %collective-permute-done.10.refs_2_), channel_id=1, source_target_pairs={{0,8},{8,0},{16,24},{24,16},{32,40},{40,32},{48,56},{56,48},{1,9},... | collective-permute-start | bytes 491528 | tf_op jit(solution)/shard_map/ppermute | solution.py:535
  54.6 4.5 %collective-permute-start.13 = (f32[320,128]{1,0:T(8,128)S(1)}, f32[320,128]{1,0:T(8,128)S(1)}, u32[]{:S(2)}, u32[]{:S(2)}) collective-permute-start(f32[320,128]{1,0:T(8,128)S(1)} %collective-permute-done.12.refs_4_), channel_id=1, source_target_pairs={{0,8},{8,0},{16,24},{24,16},{32,40},{40,32},{48,56},{56,48},{1,9},... | collective-permute-start | bytes 491528 | tf_op jit(solution)/shard_map/ppermute | solution.py:535
  57.4 2.8 %collective-permute-start.15 = (f32[320,128]{1,0:T(8,128)S(1)}, f32[320,128]{1,0:T(8,128)S(1)}, u32[]{:S(2)}, u32[]{:S(2)}) collective-permute-start(f32[320,128]{1,0:T(8,128)S(1)} %collective-permute-done.14.refs_6_), channel_id=1, source_target_pairs={{0,8},{8,0},{16,24},{24,16},{32,40},{40,32},{48,56},{56,48},{1,9},... | collective-permute-start | bytes 491528 | tf_op jit(solution)/shard_map/ppermute | solution.py:535
  65.6 5.6 %collective-permute-start.21 = (f32[88,128]{1,0:T(8,128)S(1)}, f32[88,128]{1,0:T(8,128)S(1)}, u32[]{:S(2)}, u32[]{:S(2)}) collective-permute-start(f32[88,128]{1,0:T(8,128)S(1)} %get-tuple-element.63.refs_0_), channel_id=1, source_target_pairs={{0,48},{8,56},{16,32},{24,40},{32,16},{40,24},{48,0},{56,8},{1,49}... | collective-permute-start | bytes 135176 | tf_op jit(solution)/shard_map/ppermute | solution.py:535
  67.1 5.6 %collective-permute-start.19 = (f32[88,128]{1,0:T(8,128)S(1)}, f32[88,128]{1,0:T(8,128)S(1)}, u32[]{:S(2)}, u32[]{:S(2)}) collective-permute-start(f32[88,128]{1,0:T(8,128)S(1)} %get-tuple-element.63.refs_0_), channel_id=1, source_target_pairs={{0,32},{8,40},{16,48},{24,56},{32,0},{40,8},{48,16},{56,24},{1,33}... | collective-permute-start | bytes 135176 | tf_op jit(solution)/shard_map/ppermute | solution.py:535
  67.7 6.6 %collective-permute-start.17 = (f32[88,128]{1,0:T(8,128)S(1)}, f32[88,128]{1,0:T(8,128)S(1)}, u32[]{:S(2)}, u32[]{:S(2)}) collective-permute-start(f32[88,128]{1,0:T(8,128)S(1)} %get-tuple-element.63.refs_0_), channel_id=1, source_target_pairs={{0,16},{8,24},{16,0},{24,8},{32,48},{40,56},{48,32},{56,40},{1,17}... | collective-permute-start | bytes 135176 | tf_op jit(solution)/shard_map/ppermute | solution.py:535
  68.9 6.5 %collective-permute-start.16 = (f32[88,128]{1,0:T(8,128)S(1)}, f32[88,128]{1,0:T(8,128)S(1)}, u32[]{:S(2)}, u32[]{:S(2)}) collective-permute-start(f32[88,128]{1,0:T(8,128)S(1)} %get-tuple-element.63.refs_0_), channel_id=1, source_target_pairs={{0,8},{8,0},{16,24},{24,16},{32,40},{40,32},{48,56},{56,48},{1,9},... | collective-permute-start | bytes 135176 | tf_op jit(solution)/shard_map/ppermute | solution.py:535
  71.2 4.3 %collective-permute-start.22 = (f32[88,128]{1,0:T(8,128)S(1)}, f32[88,128]{1,0:T(8,128)S(1)}, u32[]{:S(2)}, u32[]{:S(2)}) collective-permute-start(f32[88,128]{1,0:T(8,128)S(1)} %collective-permute-done.21.refs_6_), channel_id=1, source_target_pairs={{0,8},{8,0},{16,24},{24,16},{32,40},{40,32},{48,56},{56,48},{1,9},... | collective-permute-start | bytes 135176 | tf_op jit(solution)/shard_map/ppermute | solution.py:535
  72.7 2.8 %collective-permute-start.20 = (f32[88,128]{1,0:T(8,128)S(1)}, f32[88,128]{1,0:T(8,128)S(1)}, u32[]{:S(2)}, u32[]{:S(2)}) collective-permute-start(f32[88,128]{1,0:T(8,128)S(1)} %collective-permute-done.19.refs_4_), channel_id=1, source_target_pairs={{0,8},{8,0},{16,24},{24,16},{32,40},{40,32},{48,56},{56,48},{1,9},... | collective-permute-start | bytes 135176 | tf_op jit(solution)/shard_map/ppermute | solution.py:535
  74.3 1.2 %collective-permute-start.18 = (f32[88,128]{1,0:T(8,128)S(1)}, f32[88,128]{1,0:T(8,128)S(1)}, u32[]{:S(2)}, u32[]{:S(2)}) collective-permute-start(f32[88,128]{1,0:T(8,128)S(1)} %collective-permute-done.17.refs_2_), channel_id=1, source_target_pairs={{0,8},{8,0},{16,24},{24,16},{32,40},{40,32},{48,56},{56,48},{1,9},... | collective-permute-start | bytes 135176 | tf_op jit(solution)/shard_map/ppermute | solution.py:535
  (19 other events, 102.4 us)
